TPU v7x, 256 devices: a whole 4x4x8 slice. The times are simulated.
256 devices in a mesh: head: 8 (over x, core), batch: 32 (over z, y).
Axes of the slice: x: 4, y: 4, z: 8, core: 2. Of those that a mesh axis runs over, the one named last changes fastest.
Arguments:
- queries: bfloat16 [2048, 4096], P('batch', 'head'), may hold values from -6 to 6
- key_page_cache: bfloat16 [16384, 16, 1024], P('batch', None, 'head'), may hold values from -6 to 6
- value_page_cache: bfloat16 [16384, 16, 1024], P('batch', None, 'head'), may hold values from -6 to 6
- shard_page_index: int32 [32, 512], P('batch'), may hold values from 0 to 511, each once within a row
- sequence_page_count: int32 [32, 64], P('batch'), may hold values from 1 to 64, 512 in all within a row
- last_page_tokens: int32 [2048], P('batch'), may hold values from 1 to 16
- sequence_adapter_entry: int32 [2048], P('batch'), may hold values from 0 to 31
- batch_adapters: int32 [32, 32], P('batch'), may hold values from 0 to 511, as said below
- output_projection_weight: bfloat16 [4096, 4096], P('head'), may hold values from -1.5 to 1.5
- adapter_down_weight: bfloat16 [512, 4096, 64], P('batch', 'head'), may hold values from -1.5 to 1.5
- adapter_up_weight: bfloat16 [512, 64, 4096], P('batch', None, 'head'), may hold values from -0.75 to 0.75
Outputs:
- attention_out: bfloat16 [2048, 4096], P('batch', 'head')
Inputs may be any that keep to these rules, and one draw needn't show every extreme that they name: `sequence_page_count`: each row sums to 512. `batch_adapters`: each row holds 32 different ids; at most 2 of a row lie in one aligned range of 16 ids, and exactly 2 in some range; entries may be used by no sequence.
All inputs are finite; a program needn't handle non-finite values.
Results may differ from a plain program's by a relative error of at most 0.013.
Values may be sent and summed in bfloat16 or wider, within the bound.
No kernel may reach another device: no remote copies, remote signals or barrier semaphores. Data moves between devices by JAX's collectives and lax.ppermute only.
A program may use at most 128 MiB of HBM per device.

v0:
```python
import jax
import jax.numpy as jnp
from jax import lax
from jax.sharding import PartitionSpec as P

HQ = 32
KVH = 8
HD = 128
PAGE = 16


def from_everyone(shard, axis):
    count = lax.axis_size(axis)
    return lax.all_to_all(
        jnp.broadcast_to(shard[None], (count, *shard.shape)), axis, 0, 0, tiled=True
    )


def joined_along(blocks, dim):
    blocks = jnp.moveaxis(blocks, 0, dim)
    dims = blocks.shape
    return blocks.reshape(*dims[:dim], dims[dim] * dims[dim + 1], *dims[dim + 2 :])


def collect(shard, axis, dim):
    blocks = from_everyone(shard, axis)
    return joined_along(blocks, dim)


def attend(queries, keys, values, shard_page_index, sequence_page_count, last_page_tokens):
    rows = queries.shape[0]
    pool_pages = keys.shape[0]
    kv_heads = keys.shape[2] // HD
    groups = HQ // KVH
    page_start = jnp.cumsum(sequence_page_count) - sequence_page_count
    pool_range = jnp.arange(pool_pages, dtype=jnp.int32)
    place_match = shard_page_index[:, None] == pool_range[None, :]
    page_place = jnp.sum(jnp.where(place_match, pool_range[:, None], 0), axis=0)
    token_place = (page_place[:, None] * PAGE + jnp.arange(PAGE, dtype=jnp.int32)[None, :]).reshape(
        pool_pages * PAGE
    )
    key_flat = keys.reshape(pool_pages * PAGE, kv_heads, HD)
    value_flat = values.reshape(pool_pages * PAGE, kv_heads, HD)
    grouped = queries.reshape(rows, kv_heads, groups, HD)
    scores = jnp.einsum(
        "skgd,tkd->skgt", grouped, key_flat, preferred_element_type=jnp.float32
    ) * HD ** (-0.5)
    context = (sequence_page_count - 1) * PAGE + last_page_tokens
    lower = page_start * PAGE
    live_mask = (token_place[None, :] >= lower[:, None]) & (
        token_place[None, :] < (lower + context)[:, None]
    )
    scores = jnp.where(live_mask[:, None, None, :], scores, -1e30)
    top_score = jnp.max(scores, axis=-1, keepdims=True)
    powers = jnp.exp(scores - top_score)
    weights = (powers / jnp.sum(powers, axis=-1, keepdims=True)).astype(jnp.bfloat16)
    mixed = jnp.einsum("skgt,tkd->skgd", weights, value_flat, preferred_element_type=jnp.float32)
    return mixed.astype(jnp.bfloat16).reshape(rows, kv_heads * groups * HD)


def per_device(
    queries,
    key_page_cache,
    value_page_cache,
    shard_page_index,
    sequence_page_count,
    last_page_tokens,
    sequence_adapter_entry,
    batch_adapters,
    output_projection_weight,
    adapter_down_weight,
    adapter_up_weight,
):
    attention = attend(
        queries,
        key_page_cache,
        value_page_cache,
        shard_page_index[0],
        sequence_page_count[0],
        last_page_tokens,
    )
    rows = attention.shape[0]
    my_index = lax.axis_index("batch")
    peers = lax.axis_size("batch")
    count_each_shard = adapter_down_weight.shape[0]
    adapter_rank_width = adapter_down_weight.shape[2]
    output_width = adapter_up_weight.shape[2]
    need = batch_adapters.shape[1]
    own_list = batch_adapters[0]
    slot_match = sequence_adapter_entry[:, None] == jnp.arange(need, dtype=jnp.int32)[None, :]
    lists = collect(batch_adapters, "batch", 0)
    slot_cap = 2 * need // peers
    mine = (lists // count_each_shard == my_index).astype(jnp.int32)
    before = jnp.cumsum(mine, axis=1) - mine
    slot_range = jnp.arange(slot_cap, dtype=jnp.int32)
    select = (mine[:, None, :] == 1) & (before[:, None, :] == slot_range[None, :, None])
    shard_local_numbers = jnp.sum(
        jnp.where(select, (lists % count_each_shard)[:, None, :], 0), axis=-1
    )
    filled = jnp.any(select, axis=-1)
    stored_range = jnp.arange(count_each_shard, dtype=jnp.int32)
    one_hot = (
        (shard_local_numbers[:, :, None] == stored_range[None, None, :]) & filled[:, :, None]
    ).astype(jnp.bfloat16)
    send_shrink = jnp.einsum(
        "bcn,nkr->bckr", one_hot, adapter_down_weight, preferred_element_type=jnp.float32
    ).astype(jnp.bfloat16)
    send_expand = jnp.einsum(
        "bcn,nrw->bcrw", one_hot, adapter_up_weight, preferred_element_type=jnp.float32
    ).astype(jnp.bfloat16)
    got_shrink, got_expand = (
        lax.all_to_all(send_shrink, "batch", split_axis=0, concat_axis=0, tiled=True),
        lax.all_to_all(send_expand, "batch", split_axis=0, concat_axis=0, tiled=True),
    )
    my_home = own_list // count_each_shard
    order_range = jnp.arange(need, dtype=jnp.int32)
    same_home = (my_home[:, None] == my_home[None, :]) & (
        order_range[None, :] < order_range[:, None]
    )
    arrival = my_home * slot_cap + jnp.sum(same_home, axis=1)
    seq_arrival = jnp.sum(jnp.where(slot_match, arrival[None, :], 0), axis=1)
    total_slots = peers * slot_cap
    picked = seq_arrival[:, None] == jnp.arange(total_slots, dtype=jnp.int32)[None, :]
    flat_shrink = got_shrink.reshape(total_slots, got_shrink.shape[2], adapter_rank_width)
    per_slot = jnp.einsum("sk,nkr->snr", attention, flat_shrink, preferred_element_type=jnp.float32)
    shrink_part = jnp.sum(per_slot * picked.astype(jnp.float32)[:, :, None], axis=1)
    ranked = lax.psum(shrink_part, "head").astype(jnp.bfloat16)
    spread = (ranked[:, None, :] * picked.astype(jnp.bfloat16)[:, :, None]).reshape(
        rows, total_slots * adapter_rank_width
    )
    grown = jnp.dot(
        spread,
        got_expand.reshape(total_slots * adapter_rank_width, output_width),
        preferred_element_type=jnp.float32,
    )
    base_part = jnp.dot(attention, output_projection_weight, preferred_element_type=jnp.float32)
    base = lax.psum_scatter(
        base_part.astype(jnp.bfloat16), "head", scatter_dimension=1, tiled=True
    ).astype(jnp.float32)
    return (base + grown).astype(jnp.bfloat16)


def solution(mesh):
    in_specs = (
        P("batch", "head"),
        P("batch", None, "head"),
        P("batch", None, "head"),
        P("batch", None),
        P("batch", None),
        P("batch"),
        P("batch"),
        P("batch", None),
        P("head", None),
        P("batch", "head", None),
        P("batch", None, "head"),
    )
    out_specs = P("batch", "head")
    return jax.shard_map(
        per_device, mesh=mesh, in_specs=in_specs, out_specs=out_specs, check_vma=False
    )
```

profile of v0, /device:TPU:32, one launch (start us, length us, event | category | flops | bytes accessed | tf_op | source)
XLA Modules:
  0.0 246.0 jit_solution(5123666635454430823)
XLA Ops:
  6.5 1.4 broadcast_in_dim.61
  8.0 11.4 %all-to-all-start = ((s32[32,1,32]{2,1,0:T(1,128)}), s32[32,1,32]{2,1,0:T(1,128)S(1)}, u32[]{:S(2)}, u32[]{:S(2)}) async-start(s32[32,1,32]{2,1,0:T(1,128)} %broadcast_in_dim.61), calls=%async_computation.1 | async-start | bytes 32768 | tf_op jit(solution)/shard_map/all_to_all | solution.py:14
  19.3 8.5 %all-to-all-done = s32[32,1,32]{2,1,0:T(1,128)S(1)} async-done(((s32[32,1,32]{2,1,0:T(1,128)}), s32[32,1,32]{2,1,0:T(1,128)S(1)}, u32[]{:S(2)}, u32[]{:S(2)}) %all-to-all-start) | async-done | bytes 4128 | tf_op jit(solution)/shard_map/all_to_all | solution.py:14
  28.3 2.5 %convolution_convert_fusion.2 = bf16[32,2,512,64]{2,0,3,1:T(8,128)(2,1)S(1)} fusion(bf16[16,512,64]{1,2,0:T(8,128)(2,1)} %param.20, s32[32,2]{0,1:T(2,128)S(1)} %select_reduce_fusion.1, pred[32,2]{0,1:T(4,128)(4,1)S(1)} %fusion.23), kind=kOutput, calls=%fused_computation.10 | convolution fusion | flops 69208064 | bytes 5243200 | tf_op jit(solution)/shard_map/bcn,nkr->bckr/dot_general | solution.py:105
  30.8 4.4 %copy.45 = bf16[32,2,512,64]{2,3,1,0:T(8,128)(2,1)} copy(bf16[32,2,512,64]{2,0,3,1:T(8,128)(2,1)S(1)} %convolution_convert_fusion.2) | data formatting | bytes 8388608 | tf_op jit(solution)/shard_map/convert_element_type | solution.py:107
  35.2 6.0 %all-to-all-start.1 = ((bf16[32,2,512,64]{2,3,1,0:T(8,128)(2,1)}), bf16[32,2,512,64]{2,3,1,0:T(8,128)(2,1)}, u32[]{:S(2)}, u32[]{:S(2)}) async-start(bf16[32,2,512,64]{2,3,1,0:T(8,128)(2,1)} %copy.45), calls=%async_computation.2 | async-start | bytes 8388608 | tf_op jit(solution)/shard_map/all_to_all | solution.py:112
  41.2 1.3 convolution_convert_fusion.1
  42.5 4.3 %copy.48 = bf16[32,2,64,512]{3,2,1,0:T(8,128)(2,1)} copy(bf16[32,2,64,512]{3,0,2,1:T(8,128)(2,1)S(1)} %convolution_convert_fusion.1) | data formatting | bytes 8388608 | tf_op jit(solution)/shard_map/convert_element_type | solution.py:110
  46.9 87.7 %all-to-all-done.1 = bf16[32,2,512,64]{2,3,1,0:T(8,128)(2,1)} async-done(((bf16[32,2,512,64]{2,3,1,0:T(8,128)(2,1)}), bf16[32,2,512,64]{2,3,1,0:T(8,128)(2,1)}, u32[]{:S(2)}, u32[]{:S(2)}) %all-to-all-start.1) | async-done | bytes 4194336 | tf_op jit(solution)/shard_map/all_to_all | solution.py:112
  134.5 7.0 %all-to-all-start.2 = ((bf16[32,2,64,512]{3,2,1,0:T(8,128)(2,1)}), bf16[32,2,64,512]{3,2,1,0:T(8,128)(2,1)}, u32[]{:S(2)}, u32[]{:S(2)}) async-start(bf16[32,2,64,512]{3,2,1,0:T(8,128)(2,1)} %copy.48), calls=%async_computation.3 | async-start | bytes 8388608 | tf_op jit(solution)/shard_map/all_to_all | solution.py:113
  141.5 0.2 reduce-scatter.2.cloned.1.call-start
  142.6 0.5 compare_and_fusion
  143.1 1.7 fusion.44
  144.8 1.4 fusion.2
  146.1 0.2 copy-done.7
  146.4 2.0 fusion.9
  148.6 1.7 convolution_convert_fusion
  150.7 4.3 %multiply_reduce_fusion = f32[64,64]{1,0:T(8,128)S(1)} fusion(bf16[64,512,1]{1,0,2:T(8,128)(2,1)S(1)} %reshape.244, bf16[64,512,64]{1,2,0:T(8,128)(2,1)} %bitcast.24, f32[64,64]{0,1:T(8,128)S(1)} %get-tuple-element.9), kind=kOutput, calls=%fused_computation.11 | convolution fusion | flops 268955648 | bytes 4292608 | tf_op jit(solution)/shard_map/sk,nkr->snr/dot_general | solution.py:125
  155.1 25.9 %psum.7 = bf16[64,64]{1,0:T(8,128)(2,1)S(1)} all-reduce(f32[64,64]{1,0:T(8,128)S(1)} %multiply_reduce_fusion), channel_id=1, replica_groups=mesh['head'=8,'batch'=32] {'head'}, use_global_device_ids=true, to_apply=%region_11.12 | all-reduce | flops 4096 | bytes 24576 | tf_op jit(solution)/shard_map/psum | solution.py:127
  181.0 0.6 broadcast_multiply_fusion
  181.6 1.7 mul.86
  183.2 2.9 %reduce-scatter.2.cloned.1.call-done = bf16[64,512]{1,0:T(8,128)(2,1)} async-done(((bf16[64,4096]{1,0:T(8,128)(2,1)}), bf16[64,512]{1,0:T(8,128)(2,1)}) %reduce-scatter.2.cloned.1.call-update) | async-done | bytes 65552 | tf_op jit(solution)/shard_map/reduce_scatter | solution.py:137
  186.2 49.2 %all-to-all-done.2 = bf16[32,2,64,512]{3,2,1,0:T(8,128)(2,1)} async-done(((bf16[32,2,64,512]{3,2,1,0:T(8,128)(2,1)}), bf16[32,2,64,512]{3,2,1,0:T(8,128)(2,1)}, u32[]{:S(2)}, u32[]{:S(2)}) %all-to-all-start.2) | async-done | bytes 4194336 | tf_op jit(solution)/shard_map/all_to_all | solution.py:113
  235.4 3.8 %fusion.5 = bf16[64,512]{1,0:T(8,128)(2,1)} fusion(bf16[64,4096]{1,0:T(8,128)(2,1)} %mul.86, bf16[4096,512]{1,0:T(8,128)(2,1)} %bitcast.30, bf16[64,512]{1,0:T(8,128)(2,1)} %reduce-scatter.2.cloned.1.call-done), kind=kOutput, calls=%fused_computation.14 | convolution fusion | flops 268533760 | bytes 4849664 | tf_op jit(solution)/shard_map/dot_general | solution.py:131
  (42 shorter events, 1.9 us)
Async XLA Ops:
  6.5 136.5 %copy-start = (bf16[512,16,128]{2,1,0:T(8,128)(2,1)S(1)}, bf16[512,16,128]{2,1,0:T(8,128)(2,1)}, u32[]{:S(2)}) copy-start(bf16[512,16,128]{2,1,0:T(8,128)(2,1)} %param.12) | copy-start | bytes 6291460
  8.0 19.9 %all-to-all-start = ((s32[32,1,32]{2,1,0:T(1,128)}), s32[32,1,32]{2,1,0:T(1,128)S(1)}, u32[]{:S(2)}, u32[]{:S(2)}) async-start(s32[32,1,32]{2,1,0:T(1,128)} %broadcast_in_dim.61), calls=%async_computation.1 | async-start | bytes 32768 | tf_op jit(solution)/shard_map/all_to_all | solution.py:14
  35.2 6.0 %copy-start.2 = (bf16[16,64,512]{2,1,0:T(8,128)(2,1)S(1)}, bf16[16,64,512]{2,1,0:T(8,128)(2,1)}, u32[]{:S(2)}) copy-start(bf16[16,64,512]{2,1,0:T(8,128)(2,1)} %param.21) | copy-start | bytes 3145732
  35.2 99.3 %all-to-all-start.1 = ((bf16[32,2,512,64]{2,3,1,0:T(8,128)(2,1)}), bf16[32,2,512,64]{2,3,1,0:T(8,128)(2,1)}, u32[]{:S(2)}, u32[]{:S(2)}) async-start(bf16[32,2,512,64]{2,3,1,0:T(8,128)(2,1)} %copy.45), calls=%async_computation.2 | async-start | bytes 8388608 | tf_op jit(solution)/shard_map/all_to_all | solution.py:112
  46.8 94.9 %copy-start.4 = (s32[1,512]{1,0:T(1,128)S(1)}, s32[1,512]{1,0:T(1,128)}, u32[]{:S(2)}) copy-start(s32[1,512]{1,0:T(1,128)} %param.14) | copy-start | bytes 6148
  46.9 95.4 %copy-start.3 = (s32[1,64]{1,0:T(1,128)S(1)}, s32[1,64]{1,0:T(1,128)}, u32[]{:S(2)}) copy-start(s32[1,64]{1,0:T(1,128)} %param.15) | copy-start | bytes 772
  46.9 95.7 %copy-start.5 = (s32[64]{0:T(128)S(1)}, s32[64]{0:T(128)}, u32[]{:S(2)}) copy-start(s32[64]{0:T(128)} %param.16) | copy-start | bytes 772
  46.9 96.2 %copy-start.8 = (bf16[64,512]{1,0:T(8,128)(2,1)S(1)}, bf16[64,512]{1,0:T(8,128)(2,1)}, u32[]{:S(2)}) copy-start(bf16[64,512]{1,0:T(8,128)(2,1)} %param.11) | copy-start | bytes 196612
  134.5 100.8 %all-to-all-start.2 = ((bf16[32,2,64,512]{3,2,1,0:T(8,128)(2,1)}), bf16[32,2,64,512]{3,2,1,0:T(8,128)(2,1)}, u32[]{:S(2)}, u32[]{:S(2)}) async-start(bf16[32,2,64,512]{3,2,1,0:T(8,128)(2,1)} %copy.48), calls=%async_computation.3 | async-start | bytes 8388608 | tf_op jit(solution)/shard_map/all_to_all | solution.py:113
  141.5 44.6 %reduce-scatter.2.cloned.1.call-start = ((), (), s32[]{:S(2)}) async-start(), calls=%async_computation.4 | async-start | bytes 589824 | tf_op jit(solution)/shard_map/reduce_scatter | solution.py:137
  144.8 1.6 copy-start.7
  146.4 2.2 copy-start.1
  148.3 1.9 copy-start.6
  148.3 2.2 copy-start.9
Sparse Core Ops, SparseCore 0:
  150.4 35.7 reduce-scatter.1
where the time goes:
time: 247 us; the launch traced here: 246 us
  waiting for transfers between devices  148 us (60%)
  blocking collectives  25.9 us (10%)
  starting transfers between devices  24.6 us (10%)
  matrix products  17.2 us (7%)
  between operations  13.6 us (6%)
  local copies, waits for them, and re-layouts  12.6 us (5%)
  other arithmetic  3.73 us (2%)
    all_to_all x1, waiting for transfers between devices, per_device(): lax.all_to_all(send_shrink, 'batch', split_axis=0, concat_axis=0, tiled=T...  87.7 us
    all_to_all x1, waiting for transfers between devices, per_device(): lax.all_to_all(send_expand, 'batch', split_axis=0, concat_axis=0, tiled=T...  49.2 us
    psum x1, blocking collectives, per_device(): ranked = lax.psum(shrink_part, 'head').astype(jnp.bfloat16)  25.9 us
    all_to_all x1, starting transfers between devices, from_everyone(): lax.all_to_all(jnp.broadcast_to(shard[None], (count, *shard.shape)), axis...  11.4 us
    all_to_all x1, waiting for transfers between devices, from_everyone(): lax.all_to_all(jnp.broadcast_to(shard[None], (count, *shard.shape)), axis...  8.51 us
    all_to_all x1, starting transfers between devices, per_device(): lax.all_to_all(send_expand, 'batch', split_axis=0, concat_axis=0, tiled=T...  6.99 us
    all_to_all x1, starting transfers between devices, per_device(): lax.all_to_all(send_shrink, 'batch', split_axis=0, concat_axis=0, tiled=T...  6.01 us
  transfers between devices with their start and end apart: 4, of which 4 were waited for; matrix products, arithmetic and copies ran while one was open for 8% of the time, Pallas kernels for 0%

commit v1 on v0

--- a/solution.py
+++ b/solution.py
@@ -7,6 +7,8 @@
 KVH = 8
 HD = 128
 PAGE = 16
+BLOCK = 16
+HOME_ROWS = 128
 
 
 def from_everyone(shard, axis):
@@ -58,27 +60,13 @@
     return mixed.astype(jnp.bfloat16).reshape(rows, kv_heads * groups * HD)
 
 
-def per_device(
-    queries,
-    key_page_cache,
-    value_page_cache,
-    shard_page_index,
-    sequence_page_count,
-    last_page_tokens,
-    sequence_adapter_entry,
-    batch_adapters,
-    output_projection_weight,
-    adapter_down_weight,
-    adapter_up_weight,
+def exchange(blocks, axis):
+    return lax.all_to_all(blocks, axis, split_axis=0, concat_axis=0, tiled=True)
+
+
+def grown_by_moving_maps(
+    attention, sequence_adapter_entry, batch_adapters, adapter_down_weight, adapter_up_weight
 ):
-    attention = attend(
-        queries,
-        key_page_cache,
-        value_page_cache,
-        shard_page_index[0],
-        sequence_page_count[0],
-        last_page_tokens,
-    )
     rows = attention.shape[0]
     my_index = lax.axis_index("batch")
     peers = lax.axis_size("batch")
@@ -108,10 +96,7 @@
     send_expand = jnp.einsum(
         "bcn,nrw->bcrw", one_hot, adapter_up_weight, preferred_element_type=jnp.float32
     ).astype(jnp.bfloat16)
-    got_shrink, got_expand = (
-        lax.all_to_all(send_shrink, "batch", split_axis=0, concat_axis=0, tiled=True),
-        lax.all_to_all(send_expand, "batch", split_axis=0, concat_axis=0, tiled=True),
-    )
+    got_shrink, got_expand = exchange(send_shrink, "batch"), exchange(send_expand, "batch")
     my_home = own_list // count_each_shard
     order_range = jnp.arange(need, dtype=jnp.int32)
     same_home = (my_home[:, None] == my_home[None, :]) & (
@@ -128,16 +113,115 @@
     spread = (ranked[:, None, :] * picked.astype(jnp.bfloat16)[:, :, None]).reshape(
         rows, total_slots * adapter_rank_width
     )
-    grown = jnp.dot(
+    return jnp.dot(
         spread,
         got_expand.reshape(total_slots * adapter_rank_width, output_width),
         preferred_element_type=jnp.float32,
     )
-    base_part = jnp.dot(attention, output_projection_weight, preferred_element_type=jnp.float32)
-    base = lax.psum_scatter(
-        base_part.astype(jnp.bfloat16), "head", scatter_dimension=1, tiled=True
-    ).astype(jnp.float32)
-    return (base + grown).astype(jnp.bfloat16)
+
+
+def per_device(
+    queries,
+    key_page_cache,
+    value_page_cache,
+    shard_page_index,
+    sequence_page_count,
+    last_page_tokens,
+    sequence_adapter_entry,
+    batch_adapters,
+    output_projection_weight,
+    adapter_down_weight,
+    adapter_up_weight,
+):
+    f32, bf16, i32 = jnp.float32, jnp.bfloat16, jnp.int32
+    rows, width = queries.shape
+    peers = lax.axis_size("batch")
+    heads = lax.axis_size("head")
+    stored, _, rank_width = adapter_down_weight.shape
+    need = batch_adapters.shape[1]
+    output_width = adapter_up_weight.shape[2]
+    slots = peers * BLOCK
+
+    own_list = batch_adapters[0]
+    listed = sequence_adapter_entry[:, None] == jnp.arange(need, dtype=i32)[None, :]
+    ids = jnp.sum(jnp.where(listed, own_list[None, :], 0), axis=1)
+    home, local = ids // stored, ids % stored
+    order = jnp.arange(rows, dtype=i32)
+    place = jnp.sum((home[:, None] == home[None, :]) & (order[None, :] < order[:, None]), axis=1, dtype=i32)
+    fits = place < BLOCK - 1
+    slot = jnp.where(fits, home * BLOCK + place, -1)
+    pair_over = jnp.any(~fits)
+    picked = jnp.arange(slots, dtype=i32)[:, None] == slot[None, :]
+    slot_local = jnp.sum(jnp.where(picked, local[None, :] + 1, 0), axis=1).reshape(peers, BLOCK)
+    lane = jnp.arange(BLOCK, dtype=i32)
+    header = jnp.where(lane[None, :] == BLOCK - 1, pair_over.astype(i32), slot_local)
+    header = jnp.pad(header, ((0, 0), (0, width - BLOCK))).astype(bf16)
+
+    attention = attend(
+        queries,
+        key_page_cache,
+        value_page_cache,
+        shard_page_index[0],
+        sequence_page_count[0],
+        last_page_tokens,
+    )
+    send = jnp.dot(picked.astype(bf16), attention, preferred_element_type=f32).astype(bf16)
+    send = send.reshape(peers, BLOCK, width)
+    send = jnp.where(lane[None, :, None] == BLOCK - 1, header[:, None, :], send)
+    got = exchange(send, "batch")
+
+    base_part = jnp.dot(attention, output_projection_weight, preferred_element_type=f32).astype(bf16)
+    got_header = got[:, BLOCK - 1, :BLOCK].astype(f32).astype(i32)
+    any_pair_over = jnp.max(got_header[:, BLOCK - 1]) > 0
+    got_local = jnp.where(lane[None, :] == BLOCK - 1, 0, got_header).reshape(slots) - 1
+    filled = got_local >= 0
+    upto = jnp.arange(slots, dtype=i32)
+    at = jnp.sum((upto[None, :] < upto[:, None]) & filled[None, :], axis=1, dtype=i32)
+    home_over = jnp.sum(filled, dtype=i32) > HOME_ROWS
+    at = jnp.where(filled, at, -1)
+    closing = jnp.arange(HOME_ROWS, dtype=i32)[:, None] == at[None, :]
+    closed = jnp.dot(closing.astype(bf16), got.reshape(slots, width), preferred_element_type=f32).astype(bf16)
+    row_local = jnp.sum(jnp.where(closing, got_local[None, :], 0), axis=1)
+    uses = row_local[:, None] == jnp.arange(stored, dtype=i32)[None, :]
+    per_map = jnp.einsum("mk,nkr->mnr", closed, adapter_down_weight, preferred_element_type=f32)
+    part = jnp.sum(per_map * uses.astype(f32)[:, :, None], axis=1)
+    half = HOME_ROWS // 2
+    packed = jnp.concatenate([part[:half], part[half:]], axis=1).astype(bf16)
+
+    parts = jnp.concatenate(
+        [
+            jnp.moveaxis(base_part.reshape(rows, heads, output_width), 1, 0),
+            jnp.broadcast_to(packed[None], (heads, *packed.shape)),
+        ],
+        axis=2,
+    )
+    parts = exchange(parts, "head")
+    summed = jnp.sum(parts.astype(f32), axis=0)
+    base = summed[:, :output_width]
+    ranked = jnp.concatenate(
+        [summed[:, output_width : output_width + rank_width], summed[:, output_width + rank_width :]], axis=0
+    ).astype(bf16)
+    spread = (ranked[:, None, :] * uses.astype(bf16)[:, :, None]).reshape(HOME_ROWS, stored * rank_width)
+    grown_home = jnp.dot(
+        spread, adapter_up_weight.reshape(stored * rank_width, output_width), preferred_element_type=f32
+    ).astype(bf16)
+    back = jnp.einsum("ms,mw->sw", closing.astype(bf16), grown_home, preferred_element_type=f32).astype(bf16)
+    back = back.reshape(peers, BLOCK, output_width)
+    back = jnp.where(lane[None, :, None] == BLOCK - 1, home_over.astype(bf16), back)
+    back = exchange(back, "batch")
+
+    any_home_over = jnp.max(back[:, BLOCK - 1, 0].astype(f32)) > 0
+    grown = jnp.einsum(
+        "sr,sw->rw", picked.astype(bf16), back.reshape(slots, output_width), preferred_element_type=f32
+    )
+    grown = lax.cond(
+        any_pair_over | any_home_over,
+        lambda: grown_by_moving_maps(
+            attention, sequence_adapter_entry, batch_adapters, adapter_down_weight, adapter_up_weight
+        ),
+        lambda: grown,
+    )
+    return (base + grown).astype(bf16)
 
 
 def solution(mesh):

time: 247 us -> 101 us (0.41)
  waiting for transfers between devices: 148 us -> 39.5 us
  blocking collectives: 25.9 us -> 0 us
  other arithmetic: 3.73 us -> 17.5 us
  between operations: 13.6 us -> 2.99 us
  local copies, waits for them, and re-layouts: 12.6 us -> 3.49 us
  starting transfers between devices: 24.6 us -> 21 us
    all_to_all x3, waiting for transfers between devices: 145 us -> 39.5 us  [exchange(): return lax.all_to_all(blocks, axis, split_axis=0, concat_axis=0, tiled=True)]
    psum x1 -> x0, blocking collectives: 25.9 us -> none  [per_device(): ranked = lax.psum(shrink_part, 'head').astype(jnp.bfloat16)]
    convert_element_type x3 -> x1, local copies, waits for them, and re-layouts: 8.78 us -> 0.08 us  [per_device(): got_header = got[:, BLOCK - 1, :BLOCK].astype(f32).astype(i32)]
    dot_general x5 -> x4, matrix products: 13.6 us -> 8.17 us  [the longest x1 3.03 us: per_device(): jnp.dot(attention, output_projection_weight, preferred_element_type=f32)]
    reduce_sum x3 -> x8, other arithmetic: 0.38 us -> 4.36 us  [the longest x1 1.19 us: per_device(): summed = jnp.sum(parts.astype(f32), axis=0)]
    select_n x1 -> x4, other arithmetic: 0.01 us -> 3.91 us  [the longest x1 1.96 us: per_device(): send = jnp.where(lane[None, :, None] == BLOCK - 1, header[:, None, :], send)]
    all_to_all x3, starting transfers between devices: 24.4 us -> 21 us  [exchange(): return lax.all_to_all(blocks, axis, split_axis=0, concat_axis=0, tiled=True)]
    reduce_scatter x1 -> x0, waiting for transfers between devices: 2.93 us -> none  [per_device(): lax.psum_scatter(base_part.astype(jnp.bfloat16), 'head', scatter_dimensio...]
  transfers between devices with their start and end apart: 4 -> 3, of which waited for: 4 -> 3; matrix products, arithmetic and copies ran while one was open for 8% -> 5% of each run, Pallas kernels for 0% -> 0%
where the time goes in v1:
time: 101 us; the launch traced here: 99.8 us
  waiting for transfers between devices  39.5 us (39%)
  starting transfers between devices  21 us (21%)
  other arithmetic  17.5 us (17%)
  matrix products  15.1 us (15%)
  local copies, waits for them, and re-layouts  3.49 us (3%)
  between operations  2.99 us (3%)
    all_to_all x3, waiting for transfers between devices, exchange(): return lax.all_to_all(blocks, axis, split_axis=0, concat_axis=0, tiled=True)  39.5 us
    all_to_all x3, starting transfers between devices, exchange(): return lax.all_to_all(blocks, axis, split_axis=0, concat_axis=0, tiled=True)  21 us
    dot_general x1, matrix products, per_device(): jnp.dot(attention, output_projection_weight, preferred_element_type=f32)  3.03 us
    dot_general x1, matrix products, per_device(): jnp.einsum('ms,mw->sw', closing.astype(bf16), grown_home, preferred_eleme...  2.65 us
    dot_general x1, matrix products, attend(): jnp.einsum('skgd,tkd->skgt', grouped, key_flat, preferred_element_type=jn...  2.52 us
    unnamed x1, matrix products  2.5 us
  transfers between devices with their start and end apart: 3, of which 3 were waited for; matrix products, arithmetic and copies ran while one was open for 5% of the time, Pallas kernels for 0%

profile of v1, /device:TPU:32, one launch (start us, length us, event | category | flops | bytes accessed | tf_op | source)
XLA Modules:
  0.0 99.8 jit_solution(1783569547954301967)
XLA Ops:
  0.0 0.9 select_reduce_fusion.5
  2.7 0.9 select_reduce_fusion.2
  5.0 2.5 %fusion.66 = (f32[64,4]{0,1:T(4,128)S(1)}, f32[64,1,4,8192]{3,0,2,1:T(8,128)S(1)}) fusion(bf16[8192,128,1]{1,0,2:T(8,128)(2,1)S(1)} %bitcast.135, pred[64,8192]{1,0:T(8,128)(4,1)S(1)} %compare_and_fusion, bf16[64,512]{1,0:T(8,128)(2,1)} %param.13), kind=kOutput, calls=%fused_computation.137 | convolution fusion | flops 543162112 | bytes 11076608 | tf_op jit(solution)/shard_map/skgd,tkd->skgt/dot_general | solution.py:47
  7.6 1.4 %fusion.27 = f32[64,4]{0,1:T(4,128)S(1)} fusion(f32[64,1,4,8192]{3,0,2,1:T(8,128)S(1)} %get-tuple-element.70, f32[64,4]{0,1:T(4,128)S(1)} %get-tuple-element.69), kind=kLoop, calls=%fused_computation.57 | loop fusion | flops 4194048 | bytes 8390656 | tf_op jit(solution)/shard_map/reduce_sum | solution.py:58
  9.2 1.9 %fusion.35 = bf16[64,1,4,128]{3,0,2,1:T(8,128)(2,1)S(1)} fusion(bf16[8192,128,1]{1,0,2:T(8,128)(2,1)S(1)} %bitcast.152, f32[64,4]{0,1:T(4,128)S(1)} %fusion.27, f32[64,1,4,8192]{3,0,2,1:T(8,128)S(1)} %get-tuple-element.70, f32[64,4]{0,1:T(4,128)S(1)} %get-tuple-element.69), kind=kOutput, calls=%fused_computation.70 | convolution fusion | flops 543195136 | bytes 10553344 | tf_op jit(solution)/shard_map/skgt,tkd->skgd/dot_general | solution.py:59
  11.2 1.2 %convolution_convert_fusion.4 = bf16[512,512]{1,0:T(8,128)(2,1)} fusion(s32[64]{0:T(128)S(1)} %compare_select_fusion.9, bf16[8,8,4,128]{3,2,1,0:T(4,128)(2,1)S(1)} %bitcast.142), kind=kOutput, calls=%fused_computation.64 | convolution fusion | flops 33849344 | bytes 590080 | tf_op jit(solution)/shard_map/dot_general | solution.py:168
  13.3 2.0 %broadcast_select_fusion.1 = bf16[32,16,512]{2,1,0:T(8,128)(2,1)} fusion(bf16[32,16,512]{2,1,0:T(8,128)(2,1)} %bitcast.141, pred[16]{0:T(512)(128)(4,1)S(1)} %iota_compare_fusion.17, bf16[32,512]{1,0:T(8,128)(2,1)S(1)} %pad.5), kind=kLoop, calls=%fused_computation.80 | loop fusion | flops 262144 | bytes 1081360 | tf_op jit(solution)/shard_map/jit(_where)/select_n | solution.py:170
  15.3 11.4 %all-to-all-start.3 = ((bf16[32,16,512]{2,1,0:T(8,128)(2,1)}), bf16[32,16,512]{2,1,0:T(8,128)(2,1)}, u32[]{:S(2)}, u32[]{:S(2)}) async-start(bf16[32,16,512]{2,1,0:T(8,128)(2,1)} %broadcast_select_fusion.1), calls=%async_computation.3 | async-start | bytes 1048576 | tf_op jit(solution)/shard_map/all_to_all | solution.py:64
  26.8 3.0 %convolution_convert_fusion.2 = bf16[64,4096]{1,0:T(8,128)(2,1)S(1)} fusion(bf16[512,4096]{1,0:T(8,128)(2,1)} %param.21, bf16[8,8,4,128]{3,2,1,0:T(4,128)(2,1)S(1)} %bitcast.143), kind=kOutput, calls=%fused_computation.58 | convolution fusion | flops 268697600 | bytes 4784128 | tf_op jit(solution)/shard_map/dot_general | solution.py:173
  29.9 0.8 copy.104
  30.7 13.3 %all-to-all-done.3 = bf16[32,16,512]{2,1,0:T(8,128)(2,1)} async-done(((bf16[32,16,512]{2,1,0:T(8,128)(2,1)}), bf16[32,16,512]{2,1,0:T(8,128)(2,1)}, u32[]{:S(2)}, u32[]{:S(2)}) %all-to-all-start.3) | async-done | bytes 524320 | tf_op jit(solution)/shard_map/all_to_all | solution.py:64
  44.0 0.9 slice.36
  45.2 2.5 %fusion.31 = f32[128,1024]{0,1} fusion(bf16[512,1024]{0,1:T(8,128)(2,1)S(1)} %bitcast.136, bf16[512,512]{1,0:T(8,128)(2,1)} %bitcast.36, s32[512]{0:T(512)S(1)} %broadcast_select_fusion.2), kind=kOutput, calls=%fused_computation.68 | convolution fusion | flops 201457664 | bytes 2099200
  47.7 1.1 %multiply_reduce_fusion = bf16[128,64]{0,1:T(8,128)(2,1)S(1)} fusion(f32[128,16,64]{0,2,1:T(8,128)} %bitcast.137, f32[128,16]{0,1:T(8,128)S(1)} %get-tuple-element.65), kind=kLoop, calls=%fused_computation.78 | loop fusion | flops 253952 | bytes 548864 | tf_op jit(solution)/shard_map/reduce_sum | solution.py:187
  49.1 1.9 %pad_maximum_fusion = bf16[8,64,640]{2,1,0:T(8,128)(2,1)} fusion(bf16[8,64,128]{2,1,0:T(8,128)(2,1)S(1)} %broadcast_in_dim.235, bf16[8,64,512]{2,1,0:T(8,128)(2,1)} %bitcast.140), kind=kLoop, calls=%fused_computation.76 | loop fusion | flops 1310720 | bytes 1310720 | tf_op jit(solution)/shard_map/concatenate | solution.py:191
  51.0 4.3 %all-to-all-start.4 = ((bf16[8,64,640]{2,1,0:T(8,128)(2,1)}), bf16[8,64,640]{2,1,0:T(8,128)(2,1)}, u32[]{:S(2)}, u32[]{:S(2)}) async-start(bf16[8,64,640]{2,1,0:T(8,128)(2,1)} %pad_maximum_fusion), calls=%async_computation.4 | async-start | bytes 1310720 | tf_op jit(solution)/shard_map/all_to_all | solution.py:64
  56.6 10.5 %all-to-all-done.4 = bf16[8,64,640]{2,1,0:T(8,128)(2,1)} async-done(((bf16[8,64,640]{2,1,0:T(8,128)(2,1)}), bf16[8,64,640]{2,1,0:T(8,128)(2,1)}, u32[]{:S(2)}, u32[]{:S(2)}) %all-to-all-start.4) | async-done | bytes 655392 | tf_op jit(solution)/shard_map/all_to_all | solution.py:64
  67.1 1.2 %convert_reduce_fusion.1 = f32[64,640]{1,0:T(8,128)S(1)} fusion(bf16[8,64,640]{2,1,0:T(8,128)(2,1)} %all-to-all-done.4), kind=kLoop, calls=%fused_computation.62 | loop fusion | flops 614400 | bytes 819200 | tf_op jit(solution)/shard_map/reduce_sum | solution.py:199
  68.5 2.6 %convolution_convert_fusion.3 = bf16[512,512]{1,0:T(8,128)(2,1)} fusion(bf16[16,64,512]{2,1,0:T(8,128)(2,1)} %param.23, bf16[128,16]{0,1:T(8,128)(2,1)S(1)} %get-tuple-element.66, bf16[128,64]{0,1:T(8,128)(2,1)S(1)} %copy.73, s32[512]{0:T(512)S(1)} %broadcast_select_fusion.2), kind=kOutput, calls=%fused_computation.63 | convolution fusion | flops 201850880 | bytes 1595392 | tf_op jit(solution)/shard_map/ms,mw->sw/dot_general | solution.py:208
  71.2 1.9 %broadcast_select_fusion = bf16[32,16,512]{2,1,0:T(8,128)(2,1)} fusion(bf16[32,16,512]{2,1,0:T(8,128)(2,1)} %bitcast.139, pred[16]{0:T(512)(128)(4,1)S(1)} %iota_compare_fusion.17, bf16[]{:T(256)S(6)} %convert_element_type.174), kind=kLoop, calls=%fused_computation.79 | loop fusion | flops 262144 | bytes 1048594 | tf_op jit(solution)/shard_map/jit(_where)/select_n | solution.py:210
  73.1 5.3 %all-to-all-start.5 = ((bf16[32,16,512]{2,1,0:T(8,128)(2,1)}), bf16[32,16,512]{2,1,0:T(8,128)(2,1)}, u32[]{:S(2)}, u32[]{:S(2)}) async-start(bf16[32,16,512]{2,1,0:T(8,128)(2,1)} %broadcast_select_fusion), calls=%async_computation.5 | async-start | bytes 1048576 | tf_op jit(solution)/shard_map/all_to_all | solution.py:64
  79.8 15.7 %all-to-all-done.5 = bf16[32,16,512]{2,1,0:T(8,128)(2,1)} async-done(((bf16[32,16,512]{2,1,0:T(8,128)(2,1)}), bf16[32,16,512]{2,1,0:T(8,128)(2,1)}, u32[]{:S(2)}, u32[]{:S(2)}) %all-to-all-start.5) | async-done | bytes 524320 | tf_op jit(solution)/shard_map/all_to_all | solution.py:64
  95.5 1.3 %fusion.49 = f32[64,512]{1,0:T(8,128)S(1)} fusion(bf16[512,512]{1,0:T(8,128)(2,1)} %bitcast.43, s32[64]{0:T(128)S(1)} %compare_select_fusion.9), kind=kOutput, calls=%fused_computation.93 | convolution fusion | flops 33587200 | bytes 655616 | tf_op jit(solution)/shard_map/sr,sw->rw/dot_general | solution.py:214
  96.8 1.5 %slice_reduce_fusion = bf16[]{:T(256)} fusion(bf16[32,16,512]{2,1,0:T(8,128)(2,1)} %all-to-all-done.5), kind=kLoop, calls=%fused_computation.104 | loop fusion | flops 31 | bytes 66 | tf_op jit(solution)/shard_map/reduce_max | solution.py:213
  (50 shorter events, 6.8 us)
Async XLA Ops:
  0.0 5.0 %copy-start = (bf16[512,16,128]{2,1,0:T(8,128)(2,1)S(1)}, bf16[512,16,128]{2,1,0:T(8,128)(2,1)}, u32[]{:S(2)}) copy-start(bf16[512,16,128]{2,1,0:T(8,128)(2,1)} %param.14) | copy-start | bytes 6291460
  7.6 1.6 %copy-start.4 = (bf16[512,16,128]{2,1,0:T(8,128)(2,1)S(1)}, bf16[512,16,128]{2,1,0:T(8,128)(2,1)}, u32[]{:S(2)}) copy-start(bf16[512,16,128]{2,1,0:T(8,128)(2,1)} %param.15) | copy-start | bytes 6291460
  12.4 32.9 %copy-start.1 = (bf16[16,512,64]{1,2,0:T(8,128)(2,1)S(1)}, bf16[16,512,64]{1,2,0:T(8,128)(2,1)}, u32[]{:S(2)}) copy-start(bf16[16,512,64]{1,2,0:T(8,128)(2,1)} %param.22) | copy-start | bytes 3145732
  15.3 28.7 %all-to-all-start.3 = ((bf16[32,16,512]{2,1,0:T(8,128)(2,1)}), bf16[32,16,512]{2,1,0:T(8,128)(2,1)}, u32[]{:S(2)}, u32[]{:S(2)}) async-start(bf16[32,16,512]{2,1,0:T(8,128)(2,1)} %broadcast_select_fusion.1), calls=%async_computation.3 | async-start | bytes 1048576 | tf_op jit(solution)/shard_map/all_to_all | solution.py:64
  49.0 49.9 %copy-start.3 = (s32[1,32]{1,0:T(1,128)S(1)}, s32[1,32]{1,0:T(1,128)}, u32[]{:S(2)}) copy-start(s32[1,32]{1,0:T(1,128)} %param.20) | copy-start | bytes 388
  49.1 49.9 %copy-start.5 = (s32[64]{0:T(128)S(1)}, s32[64]{0:T(128)}, u32[]{:S(2)}) copy-start(s32[64]{0:T(128)} %param.19) | copy-start | bytes 772
  51.0 16.1 %all-to-all-start.4 = ((bf16[8,64,640]{2,1,0:T(8,128)(2,1)}), bf16[8,64,640]{2,1,0:T(8,128)(2,1)}, u32[]{:S(2)}, u32[]{:S(2)}) async-start(bf16[8,64,640]{2,1,0:T(8,128)(2,1)} %pad_maximum_fusion), calls=%async_computation.4 | async-start | bytes 1310720 | tf_op jit(solution)/shard_map/all_to_all | solution.py:64
  73.1 22.3 %all-to-all-start.5 = ((bf16[32,16,512]{2,1,0:T(8,128)(2,1)}), bf16[32,16,512]{2,1,0:T(8,128)(2,1)}, u32[]{:S(2)}, u32[]{:S(2)}) async-start(bf16[32,16,512]{2,1,0:T(8,128)(2,1)} %broadcast_select_fusion), calls=%async_computation.5 | async-start | bytes 1048576 | tf_op jit(solution)/shard_map/all_to_all | solution.py:64

commit v2 on v0

v2 whole, which is shorter than its diff:
```python
import functools

import jax
import jax.numpy as jnp
from jax import lax
from jax.experimental import pallas as pl
from jax.experimental.pallas import tpu as pltpu
from jax.sharding import PartitionSpec as P

HQ = 32
KVH = 8
HD = 128
PAGE = 16
BLOCK = 16
HOME_ROWS = 128
CHUNK = 512
F32, BF16, I32 = jnp.float32, jnp.bfloat16, jnp.int32


def iota(shape, dim):
    return lax.broadcasted_iota(I32, shape, dim)


def nn(a, b):
    return lax.dot_general(a, b, (((1,), (0,)), ((), ())), preferred_element_type=F32)


def nt(a, b):
    return lax.dot_general(a, b, (((1,), (1,)), ((), ())), preferred_element_type=F32)


def column(row):
    n = row.shape[1]
    return jnp.sum(jnp.where(iota((n, n), 0) == iota((n, n), 1), row, 0.0), axis=1, keepdims=True)


def source_kernel(
    index_ref,
    count_ref,
    last_ref,
    entry_ref,
    list_ref,
    q_ref,
    keys_hbm,
    values_hbm,
    send_ref,
    attention_ref,
    target_ref,
    keys_ref,
    values_ref,
    scores_ref,
    owner_ref,
    sems,
    *,
    stored,
    peers,
):
    rows = q_ref.shape[0]
    pages = index_ref.shape[1]
    tokens = pages * PAGE
    groups = HQ // KVH
    steps = tokens // CHUNK
    copy_keys = pltpu.make_async_copy(keys_hbm, keys_ref, sems.at[0])
    copy_values = pltpu.make_async_copy(values_hbm, values_ref, sems.at[1])
    copy_keys.start()
    copy_values.start()

    count = count_ref[...].astype(F32)
    end = jnp.sum(jnp.where(iota((rows, rows), 1) <= iota((rows, rows), 0), count, 0.0), axis=1, keepdims=True)
    last = column(last_ref[...].astype(F32))
    position = iota((rows, pages), 1).astype(F32)
    owner = jnp.sum((end <= position).astype(F32), axis=0, keepdims=True)
    limit = PAGE - jnp.sum(jnp.where(position == end - 1.0, PAGE - last, 0.0), axis=0, keepdims=True)
    index = index_ref[...]
    per_row = 128 // PAGE
    high = iota((tokens // 128, pages), 0) == index // per_row
    low = (iota((128, pages), 0) // PAGE == index % per_row).astype(F32).astype(BF16)
    owner = nt(jnp.where(high, owner, 0.0).astype(BF16), low)
    limit = nt(jnp.where(high, limit, 0.0).astype(BF16), low)
    inside = (iota((tokens // 128, 128), 1) % PAGE).astype(F32) < limit
    owner_ref[...] = jnp.where(inside, owner, -1.0)

    adapters = list_ref[...].astype(F32)
    entry = entry_ref[...].astype(F32)
    need = adapters.shape[1]
    ids_row = jnp.sum(
        jnp.where(iota((need, rows), 0).astype(F32) == entry, column(adapters), 0.0), axis=0, keepdims=True
    )
    ids_col = column(ids_row)
    home_row = ids_row.astype(I32) // stored
    home_col = ids_col.astype(I32) // stored
    local_row = ids_row.astype(I32) % stored
    same = home_col == home_row
    sub, lane = iota((rows, rows), 0), iota((rows, rows), 1)
    place_row = jnp.sum((same & (sub < lane)).astype(F32), axis=0, keepdims=True).astype(I32)
    place_col = jnp.sum((same & (lane < sub)).astype(F32), axis=1, keepdims=True).astype(I32)
    target = jnp.where(place_row < BLOCK - 1, home_row * BLOCK + place_row, -1)
    target_ref[...] = target
    over = jnp.max(place_row.astype(F32), axis=1, keepdims=True) >= BLOCK - 1
    width = q_ref.shape[1]
    heads_of = jnp.where(iota((peers, rows), 0) == home_row, local_row + 1, 0).astype(F32).astype(BF16)
    spread = (iota((rows, width), 1) % BLOCK == place_col).astype(F32).astype(BF16)
    header = nn(heads_of, spread)
    header = jnp.where(iota((peers, width), 1) % BLOCK == BLOCK - 1, over.astype(F32), header).astype(BF16)

    q = jnp.concatenate([q_ref[:, g * HD : (g + 1) * HD] for g in range(groups)], axis=0)
    own = (iota((groups * rows, 128), 0) % rows).astype(F32)
    copy_keys.wait()
    top = jnp.full((groups * rows, 128), -1e30, F32)
    for step in range(steps):
        block = nt(q, keys_ref[step * CHUNK : (step + 1) * CHUNK, :])
        for part in range(CHUNK // 128):
            at = step * (CHUNK // 128) + part
            kept = jnp.where(owner_ref[at : at + 1, :] == own, block[:, part * 128 : (part + 1) * 128], -1e30)
            scores_ref[:, at * 128 : (at + 1) * 128] = kept
            top = jnp.maximum(top, kept)
    factor = HD**-0.5 * 1.4426950408889634
    top = jnp.max(top, axis=1, keepdims=True)
    copy_values.wait()
    total = jnp.zeros((groups * rows, 128), F32)
    mixed = jnp.zeros((groups * rows, HD), F32)
    for step in range(steps):
        powers = jnp.exp2((scores_ref[:, step * CHUNK : (step + 1) * CHUNK] - top) * factor)
        for part in range(CHUNK // 128):
            total = total + powers[:, part * 128 : (part + 1) * 128]
        mixed = mixed + nn(powers.astype(BF16), values_ref[step * CHUNK : (step + 1) * CHUNK, :])
    mixed = (mixed / jnp.sum(total, axis=1, keepdims=True)).astype(BF16)
    attention = jnp.concatenate([mixed[g * rows : (g + 1) * rows] for g in range(groups)], axis=1)
    attention_ref[...] = attention

    slots = peers * BLOCK
    picked = jnp.concatenate(
        [
            (iota((slots, rows), 0) == target).astype(F32),
            (iota((slots, peers), 0) == iota((slots, peers), 1) * BLOCK + BLOCK - 1).astype(F32),
        ],
        axis=1,
    ).astype(BF16)
    send_ref[...] = nn(picked, jnp.concatenate([attention, header], axis=0)).astype(BF16)


def base_kernel(attention_ref, weight_ref, out_ref):
    out_ref[0] = nn(attention_ref[...], weight_ref[...]).astype(BF16)


def home_down_kernel(got_ref, down_ref, base_ref, parts_ref, closing_ref, local_ref, over_ref):
    slots, width = got_ref.shape
    peers = slots // BLOCK
    got = got_ref[...]
    is_header = (iota((peers, slots), 1) == iota((peers, slots), 0) * BLOCK + BLOCK - 1).astype(F32).astype(BF16)
    header = nn(is_header, got)[:, :slots]
    lane = iota((peers, slots), 1)
    sub = iota((peers, slots), 0)
    flags = jnp.where(lane % BLOCK == BLOCK - 1, header, 0.0)
    ids = jnp.where(lane % BLOCK == BLOCK - 1, 0.0, header)
    ids_first = jnp.where(lane < BLOCK, ids, 0.0)
    filled = jnp.sum((ids_first > 0.0).astype(F32), axis=1, keepdims=True)
    before = jnp.sum(jnp.where(sub < lane // BLOCK, filled, 0.0), axis=0, keepdims=True)
    here = jnp.sum(jnp.where(sub == lane // BLOCK, filled, 0.0), axis=0, keepdims=True)
    local = jnp.sum(jnp.where(sub == lane // BLOCK, ids, 0.0), axis=0, keepdims=True)
    within = (iota((1, slots), 1) % BLOCK).astype(F32)
    at = jnp.where(within < here, before + within, -1.0)
    closing = (at == iota((HOME_ROWS, slots), 0).astype(F32)).astype(F32).astype(BF16)
    closing_ref[...] = closing
    closed = nn(closing, got).astype(BF16)
    locals_ = jnp.broadcast_to(local, (HOME_ROWS, slots)).astype(BF16)
    local_ref[...] = nt(closing, locals_)
    local_lanes = nt(locals_, closing)[:1, :]
    per_map = nt(down_ref[...], closed)
    rank = per_map.shape[0] // 16
    total = jnp.zeros((rank, HOME_ROWS), F32)
    for n in range(16):
        total = total + jnp.where(local_lanes == n + 1.0, per_map[n * rank : (n + 1) * rank, :], 0.0)
    total = total.astype(BF16)
    for h in range(base_ref.shape[0]):
        parts_ref[h, :, : base_ref.shape[2]] = base_ref[h]
        parts_ref[h, :, base_ref.shape[2] :] = total
    any_pair = jnp.max(jnp.max(flags, axis=1, keepdims=True), axis=0, keepdims=True)
    served = jnp.sum(filled, axis=0, keepdims=True)
    over = jnp.maximum(any_pair, (served > HOME_ROWS).astype(F32))
    over_ref[...] = jnp.broadcast_to(over, over_ref.shape)


def home_up_kernel(parts_ref, up_ref, closing_ref, local_ref, over_ref, back_ref):
    heads, rank, wide = parts_ref.shape
    width = wide - HOME_ROWS
    slots = closing_ref.shape[1]
    total = parts_ref[0, :, width:].astype(F32)
    for h in range(1, heads):
        total = total + parts_ref[h, :, width:].astype(F32)
    ranked = jnp.concatenate([total, total], axis=0).T
    local = local_ref[...]
    stored = up_ref.shape[0] // rank
    half = iota((HOME_ROWS, 128), 1) // rank
    spread = jnp.concatenate(
        [jnp.where(local == (half + 2 * pair + 1).astype(F32), ranked, 0.0).astype(BF16) for pair in range(stored // 2)],
        axis=1,
    )
    grown = nn(spread, up_ref[...]).astype(BF16)
    opened = closing_ref[...].astype(F32).T.astype(BF16)
    back = nn(opened, grown)
    row = iota((slots, width), 0)
    back_ref[...] = jnp.where(row % BLOCK == BLOCK - 1, over_ref[:1, :1], back).astype(BF16)


def tail_kernel(back_ref, parts_ref, target_ref, out_ref, base_ref, over_ref):
    heads, rows, wide = parts_ref.shape
    slots, width = back_ref.shape
    base = parts_ref[0, :, :width].astype(F32)
    for h in range(1, heads):
        base = base + parts_ref[h, :, :width].astype(F32)
    base_ref[...] = base
    target = column(target_ref[...].astype(F32))
    picked = (iota((rows, slots), 1).astype(F32) == target).astype(F32).astype(BF16)
    back = back_ref[...]
    out_ref[...] = (base + nn(picked, back)).astype(BF16)
    peers = slots // BLOCK
    is_header = (iota((peers, slots), 1) == iota((peers, slots), 0) * BLOCK + BLOCK - 1).astype(F32).astype(BF16)
    over_ref[0, 0] = jnp.max(nn(is_header, back[:, :128]))


def call(body, outs, args, scratch=(), hbm=(), smem_out=(), flops=0):
    vmem = pl.BlockSpec(memory_space=pltpu.VMEM)
    return pl.pallas_call(
        body,
        out_shape=[jax.ShapeDtypeStruct(shape, kind) for shape, kind in outs],
        in_specs=[pl.BlockSpec(memory_space=pl.ANY) if i in hbm else vmem for i in range(len(args))],
        out_specs=[pl.BlockSpec(memory_space=pltpu.SMEM) if i in smem_out else vmem for i in range(len(outs))],
        scratch_shapes=list(scratch),
        cost_estimate=pl.CostEstimate(flops=flops, transcendentals=0, bytes_accessed=1 << 20),
    )(*args)


def from_everyone(shard, axis):
    count = lax.axis_size(axis)
    return lax.all_to_all(
        jnp.broadcast_to(shard[None], (count, *shard.shape)), axis, 0, 0, tiled=True
    )


def joined_along(blocks, dim):
    blocks = jnp.moveaxis(blocks, 0, dim)
    dims = blocks.shape
    return blocks.reshape(*dims[:dim], dims[dim] * dims[dim + 1], *dims[dim + 2 :])


def collect(shard, axis, dim):
    blocks = from_everyone(shard, axis)
    return joined_along(blocks, dim)


def exchange(blocks, axis):
    return lax.all_to_all(blocks, axis, split_axis=0, concat_axis=0, tiled=True)


def grown_by_moving_maps(
    attention, sequence_adapter_entry, batch_adapters, adapter_down_weight, adapter_up_weight
):
    rows = attention.shape[0]
    my_index = lax.axis_index("batch")
    peers = lax.axis_size("batch")
    count_each_shard = adapter_down_weight.shape[0]
    adapter_rank_width = adapter_down_weight.shape[2]
    output_width = adapter_up_weight.shape[2]
    need = batch_adapters.shape[1]
    own_list = batch_adapters[0]
    slot_match = sequence_adapter_entry[:, None] == jnp.arange(need, dtype=jnp.int32)[None, :]
    lists = collect(batch_adapters, "batch", 0)
    slot_cap = 2 * need // peers
    mine = (lists // count_each_shard == my_index).astype(jnp.int32)
    before = jnp.cumsum(mine, axis=1) - mine
    slot_range = jnp.arange(slot_cap, dtype=jnp.int32)
    select = (mine[:, None, :] == 1) & (before[:, None, :] == slot_range[None, :, None])
    shard_local_numbers = jnp.sum(
        jnp.where(select, (lists % count_each_shard)[:, None, :], 0), axis=-1
    )
    filled = jnp.any(select, axis=-1)
    stored_range = jnp.arange(count_each_shard, dtype=jnp.int32)
    one_hot = (
        (shard_local_numbers[:, :, None] == stored_range[None, None, :]) & filled[:, :, None]
    ).astype(jnp.bfloat16)
    send_shrink = jnp.einsum(
        "bcn,nkr->bckr", one_hot, adapter_down_weight, preferred_element_type=jnp.float32
    ).astype(jnp.bfloat16)
    send_expand = jnp.einsum(
        "bcn,nrw->bcrw", one_hot, adapter_up_weight, preferred_element_type=jnp.float32
    ).astype(jnp.bfloat16)
    got_shrink, got_expand = exchange(send_shrink, "batch"), exchange(send_expand, "batch")
    my_home = own_list // count_each_shard
    order_range = jnp.arange(need, dtype=jnp.int32)
    same_home = (my_home[:, None] == my_home[None, :]) & (
        order_range[None, :] < order_range[:, None]
    )
    arrival = my_home * slot_cap + jnp.sum(same_home, axis=1)
    seq_arrival = jnp.sum(jnp.where(slot_match, arrival[None, :], 0), axis=1)
    total_slots = peers * slot_cap
    picked = seq_arrival[:, None] == jnp.arange(total_slots, dtype=jnp.int32)[None, :]
    flat_shrink = got_shrink.reshape(total_slots, got_shrink.shape[2], adapter_rank_width)
    per_slot = jnp.einsum("sk,nkr->snr", attention, flat_shrink, preferred_element_type=jnp.float32)
    shrink_part = jnp.sum(per_slot * picked.astype(jnp.float32)[:, :, None], axis=1)
    ranked = lax.psum(shrink_part, "head").astype(jnp.bfloat16)
    spread = (ranked[:, None, :] * picked.astype(jnp.bfloat16)[:, :, None]).reshape(
        rows, total_slots * adapter_rank_width
    )
    return jnp.dot(
        spread,
        got_expand.reshape(total_slots * adapter_rank_width, output_width),
        preferred_element_type=jnp.float32,
    )


def per_device(
    queries,
    key_page_cache,
    value_page_cache,
    shard_page_index,
    sequence_page_count,
    last_page_tokens,
    sequence_adapter_entry,
    batch_adapters,
    output_projection_weight,
    adapter_down_weight,
    adapter_up_weight,
):
    rows, width = queries.shape
    peers = lax.axis_size("batch")
    heads = lax.axis_size("head")
    stored, _, rank = adapter_down_weight.shape
    output_width = adapter_up_weight.shape[2]
    pages = key_page_cache.shape[0]
    tokens = pages * PAGE
    slots = peers * BLOCK
    query_rows = rows * (HQ // KVH)

    send, attention, target = call(
        functools.partial(source_kernel, stored=stored, peers=peers),
        [((slots, width), BF16), ((rows, width), BF16), ((1, rows), I32)],
        [
            shard_page_index,
            sequence_page_count,
            last_page_tokens.reshape(1, rows),
            sequence_adapter_entry.reshape(1, rows),
            batch_adapters,
            queries,
            key_page_cache.reshape(tokens, HD),
            value_page_cache.reshape(tokens, HD),
        ],
        scratch=[
            pltpu.VMEM((tokens, HD), BF16),
            pltpu.VMEM((tokens, HD), BF16),
            pltpu.VMEM((query_rows, tokens), F32),
            pltpu.VMEM((tokens // 128, 128), F32),
            pltpu.SemaphoreType.DMA((2,)),
        ],
        hbm=(6, 7),
        flops=4 * query_rows * tokens * HD,
    )
    got = exchange(send.reshape(peers, BLOCK, width), "batch").reshape(slots, width)

    base = pl.pallas_call(
        base_kernel,
        grid=(heads,),
        out_shape=jax.ShapeDtypeStruct((heads, rows, output_width), BF16),
        in_specs=[
            pl.BlockSpec((rows, width), lambda h: (0, 0)),
            pl.BlockSpec((width, output_width), lambda h: (0, h)),
        ],
        out_specs=pl.BlockSpec((1, rows, output_width), lambda h: (h, 0, 0)),
        cost_estimate=pl.CostEstimate(
            flops=2 * rows * width * heads * output_width, transcendentals=0, bytes_accessed=5 << 20
        ),
    )(attention, output_projection_weight)

    wide = output_width + HOME_ROWS
    parts, closing, local, over = call(
        home_down_kernel,
        [((heads, rank, wide), BF16), ((HOME_ROWS, slots), BF16), ((HOME_ROWS, HOME_ROWS), F32), ((8, 128), F32)],
        [got, jnp.swapaxes(adapter_down_weight, 1, 2).reshape(stored * rank, width), base],
        flops=2 * HOME_ROWS * width * stored * rank,
    )
    parts = exchange(parts, "head")
    (back,) = call(
        home_up_kernel,
        [((slots, output_width), BF16)],
        [parts, adapter_up_weight.reshape(stored * rank, output_width), closing, local, over],
        flops=2 * HOME_ROWS * output_width * stored * rank,
    )
    back = exchange(back.reshape(peers, BLOCK, output_width), "batch").reshape(slots, output_width)
    out, base, over = call(
        tail_kernel,
        [((rows, output_width), BF16), ((rows, output_width), F32), ((1, 1), F32)],
        [back, parts, target],
        smem_out=(2,),
        flops=2 * rows * slots * output_width,
    )

    def moving():
        grown = grown_by_moving_maps(
            attention, sequence_adapter_entry, batch_adapters, adapter_down_weight, adapter_up_weight
        )
        return (base + grown).astype(BF16)

    return lax.cond(over[0, 0] > 0.0, moving, lambda: out)


def solution(mesh):
    in_specs = (
        P("batch", "head"),
        P("batch", None, "head"),
        P("batch", None, "head"),
        P("batch", None),
        P("batch", None),
        P("batch"),
        P("batch"),
        P("batch", None),
        P("head", None),
        P("batch", "head", None),
        P("batch", None, "head"),
    )
    out_specs = P("batch", "head")
    return jax.shard_map(
        per_device, mesh=mesh, in_specs=in_specs, out_specs=out_specs, check_vma=False
    )
```

time: 247 us -> 84.5 us (0.34)
  waiting for transfers between devices: 148 us -> 10.7 us
  Pallas kernels: 0 us -> 20.9 us
  matrix products: 17.2 us -> 0 us
  starting transfers between devices: 24.6 us -> 11.4 us
  between operations: 13.6 us -> 0.72 us
  blocking collectives: 25.9 us -> 38.6 us
  local copies, waits for them, and re-layouts: 12.6 us -> 1.46 us
  other arithmetic: 3.73 us -> 0 us
    all_to_all x3 -> x1, waiting for transfers between devices: 145 us -> 10.7 us  [exchange(): return lax.all_to_all(blocks, axis, split_axis=0, concat_axis=0, tiled=True)]
    all_to_all x0 -> x2, blocking collectives: none -> 38.6 us  [exchange(): return lax.all_to_all(blocks, axis, split_axis=0, concat_axis=0, tiled=True)]
    psum x1 -> x0, blocking collectives: 25.9 us -> none  [per_device(): ranked = lax.psum(shrink_part, 'head').astype(jnp.bfloat16)]
    pallas_call x0 -> x5, Pallas kernels: none -> 20.9 us  [the longest x4 14.4 us: call(): pl.pallas_call(body, out_shape=[jax.ShapeDtypeStruct(shape, kind) for sha...]
    dot_general x7 -> x0, matrix products: 17.2 us -> none  [the longest x1 4.31 us: per_device(): jnp.einsum('sk,nkr->snr', attention, flat_shrink, preferred_element_type=...]
    all_to_all x3 -> x1, starting transfers between devices: 24.4 us -> 11.4 us  [exchange(): return lax.all_to_all(blocks, axis, split_axis=0, concat_axis=0, tiled=True)]
    convert_element_type x4 -> x0, local copies, waits for them, and re-layouts: 8.83 us -> none  [the longest x1 4.37 us: per_device(): send_shrink = jnp.einsum('bcn,nkr->bckr', one_hot, adapter_down_weight, p...]
    reduce_scatter x1 -> x0, waiting for transfers between devices: 2.93 us -> none  [per_device(): lax.psum_scatter(base_part.astype(jnp.bfloat16), 'head', scatter_dimensio...]
  transfers between devices with their start and end apart: 4 -> 1, of which waited for: 4 -> 1; matrix products, arithmetic and copies ran while one was open for 8% -> 0% of each run, Pallas kernels for 0% -> 8%
where the time goes in v2:
time: 84.5 us; the launch traced here: 84 us
  blocking collectives  38.6 us (46%)
  Pallas kernels  20.9 us (25%)
  starting transfers between devices  11.4 us (13%)
  waiting for transfers between devices  10.7 us (13%)
  local copies, waits for them, and re-layouts  1.46 us (2%)
    all_to_all x2, blocking collectives, exchange(): return lax.all_to_all(blocks, axis, split_axis=0, concat_axis=0, tiled=True)  38.6 us
    pallas_call x4, Pallas kernels, call(): pl.pallas_call(body, out_shape=[jax.ShapeDtypeStruct(shape, kind) for sha...  14.4 us
    all_to_all x1, starting transfers between devices, exchange(): return lax.all_to_all(blocks, axis, split_axis=0, concat_axis=0, tiled=True)  11.4 us
    all_to_all x1, waiting for transfers between devices, exchange(): return lax.all_to_all(blocks, axis, split_axis=0, concat_axis=0, tiled=True)  10.7 us
    pallas_call x1, Pallas kernels, per_device(): pl.pallas_call(base_kernel, grid=(heads,), out_shape=jax.ShapeDtypeStruct...  6.49 us
  transfers between devices with their start and end apart: 1, of which 1 were waited for; matrix products, arithmetic and copies ran while one was open for 0% of the time, Pallas kernels for 8%

profile of v2, /device:TPU:32, one launch (start us, length us, event | category | flops | bytes accessed | tf_op | source)
XLA Modules:
  0.0 84.0 jit_solution(15836065093105151309)
XLA Ops:
  0.0 0.0 copy-start.1
  0.0 6.7 %shard_map.111 = (bf16[512,512]{1,0:T(8,128)(2,1)}, bf16[64,512]{1,0:T(8,128)(2,1)S(1)}, s32[1,64]{1,0:T(1,128)}) custom-call(s32[1,512]{1,0:T(1,128)} %index_ref.1, s32[1,64]{1,0:T(1,128)} %count_ref.1, s32[1,64]{1,0:T(1,128)} %bitcast.68, s32[1,64]{1,0:T(1,128)} %bitcast.69, s32[1,32]{1,0:T(1,128)} %list_ref.1, bf16[64,512]{1,0:T(8,128)(2,1)} %q_ref.1, ...), custom_call_target="tpu_custom_call" | custom-call | flops 1073741824 | bytes 1048576 | tf_op jit(solution)/shard_map/pallas_call | solution.py:224
  6.7 11.4 %all-to-all-start.3 = ((bf16[32,16,512]{2,1,0:T(8,128)(2,1)}), bf16[32,16,512]{2,1,0:T(8,128)(2,1)S(1)}, u32[]{:S(2)}, u32[]{:S(2)}) async-start(bf16[32,16,512]{2,1,0:T(8,128)(2,1)} %bitcast.64), calls=%async_computation.3 | async-start | bytes 1048576 | tf_op jit(solution)/shard_map/all_to_all | solution.py:253
  18.1 0.0 copy-start
  18.1 6.5 %shard_map.112.base_ref = bf16[8,64,512]{2,1,0:T(8,128)(2,1)} custom-call(bf16[64,512]{1,0:T(8,128)(2,1)S(1)} %get-tuple-element.38.attention_ref, bf16[512,4096]{1,0:T(8,128)(2,1)} %weight_ref.1), custom_call_target="tpu_custom_call" | custom-call | flops 268435456 | bytes 5242880 | tf_op jit(solution)/shard_map/pallas_call | solution.py:360
  24.6 0.0 copy-start.3
  24.6 0.0 copy-start.4
  24.6 10.7 %all-to-all-done.3 = bf16[32,16,512]{2,1,0:T(8,128)(2,1)S(1)} async-done(((bf16[32,16,512]{2,1,0:T(8,128)(2,1)}), bf16[32,16,512]{2,1,0:T(8,128)(2,1)S(1)}, u32[]{:S(2)}, u32[]{:S(2)}) %all-to-all-start.3) | async-done | bytes 524320 | tf_op jit(solution)/shard_map/all_to_all | solution.py:253
  35.3 0.0 copy-start.2
  35.3 0.8 copy-done.2
  36.1 0.0 copy-done.1
  36.1 3.0 %shard_map.113 = (bf16[8,64,640]{2,1,0:T(8,128)(2,1)}, bf16[128,512]{1,0:T(8,128)(2,1)}, f32[128,128]{1,0:T(8,128)}, f32[8,128]{1,0:T(8,128)}) custom-call(bf16[512,512]{1,0:T(8,128)(2,1)} %bitcast.63, bf16[1024,512]{1,0:T(8,128)(2,1)S(1)} %bitcast.58, bf16[8,64,512]{2,1,0:T(8,128)(2,1)} %shard_map.112.base_ref), custom_call_target="tpu_custom_call" | custom-call | flops 134217728 | bytes 1048576 | tf_op jit(solution)/shard_map/pallas_call | solution.py:224
  39.1 16.2 %all_to_all.27.parts_ref = bf16[8,64,640]{2,1,0:T(8,128)(2,1)} all-to-all(bf16[8,64,640]{2,1,0:T(8,128)(2,1)} %get-tuple-element.39), channel_id=1, replica_groups=mesh['head'=8,'batch'=32] {'head'}, dimensions={0} | all-to-all | bytes 1310720 | tf_op jit(solution)/shard_map/all_to_all | solution.py:253
  55.2 0.0 copy-done
  55.2 2.6 %shard_map.114 = bf16[512,512]{1,0:T(8,128)(2,1)} custom-call(bf16[8,64,640]{2,1,0:T(8,128)(2,1)} %all_to_all.27.parts_ref, bf16[1024,512]{1,0:T(8,128)(2,1)S(1)} %bitcast.57, bf16[128,512]{1,0:T(8,128)(2,1)} %get-tuple-element.40.closing_ref, f32[128,128]{1,0:T(8,128)} %get-tuple-element.41.local_ref, f32[8,128]{1,0:T(8,128)} %get-tuple-element.42.over_ref), custom_call_target="tpu_custom_call" | custom-call | flops 134217728 | bytes 1048576 | tf_op jit(solution)/shard_map/pallas_call | solution.py:224
  57.8 22.4 %all_to_all.28 = bf16[32,16,512]{2,1,0:T(8,128)(2,1)} all-to-all(bf16[32,16,512]{2,1,0:T(8,128)(2,1)} %bitcast.61), channel_id=1, replica_groups=mesh['head'=8,'batch'=32] {'batch'}, dimensions={0} | all-to-all | bytes 1048576 | tf_op jit(solution)/shard_map/all_to_all | solution.py:253
  80.3 2.2 %shard_map.115 = (bf16[64,512]{1,0:T(8,128)(2,1)S(1)}, f32[64,512]{1,0:T(8,128)S(1)}, f32[1,1]{1,0:T(1,128)}) custom-call(bf16[512,512]{1,0:T(8,128)(2,1)} %bitcast.62, bf16[8,64,640]{2,1,0:T(8,128)(2,1)} %all_to_all.27.parts_ref, s32[1,64]{1,0:T(1,128)} %get-tuple-element.43.target_ref), custom_call_target="tpu_custom_call" | custom-call | flops 33554432 | bytes 1048576 | tf_op jit(solution)/shard_map/pallas_call | solution.py:224
  83.1 0.0 copy-done.3
  83.1 0.0 copy-done.4
  83.1 0.2 conditional.1
  83.3 0.0 copy-start.5
  83.3 0.6 copy-done.5
Async XLA Ops:
  0.0 36.1 %copy-start.1 = (bf16[16,512,64]{1,2,0:T(8,128)(2,1)S(1)}, bf16[16,512,64]{1,2,0:T(8,128)(2,1)}, u32[]{:S(2)}) copy-start(bf16[16,512,64]{1,2,0:T(8,128)(2,1)} %param.22) | copy-start | bytes 3145732
  6.7 28.6 %all-to-all-start.3 = ((bf16[32,16,512]{2,1,0:T(8,128)(2,1)}), bf16[32,16,512]{2,1,0:T(8,128)(2,1)S(1)}, u32[]{:S(2)}, u32[]{:S(2)}) async-start(bf16[32,16,512]{2,1,0:T(8,128)(2,1)} %bitcast.64), calls=%async_computation.3 | async-start | bytes 1048576 | tf_op jit(solution)/shard_map/all_to_all | solution.py:253
  18.1 37.1 %copy-start = (bf16[16,64,512]{2,1,0:T(8,128)(2,1)S(1)}, bf16[16,64,512]{2,1,0:T(8,128)(2,1)}, u32[]{:S(2)}) copy-start(bf16[16,64,512]{2,1,0:T(8,128)(2,1)} %param.23) | copy-start | bytes 3145732
  24.6 58.5 %copy-start.3 = (s32[1,32]{1,0:T(1,128)S(1)}, s32[1,32]{1,0:T(1,128)}, u32[]{:S(2)}) copy-start(s32[1,32]{1,0:T(1,128)} %list_ref.1) | copy-start | bytes 388
  24.6 58.5 %copy-start.4 = (s32[64]{0:T(128)S(1)}, s32[64]{0:T(128)}, u32[]{:S(2)}) copy-start(s32[64]{0:T(128)} %param.19) | copy-start | bytes 772
  35.3 0.8 copy-start.2
  83.3 0.6 copy-start.5

commit v3 on v2

--- a/solution.py
+++ b/solution.py
@@ -216,18 +216,19 @@
     out_ref[...] = (base + nn(picked, back)).astype(BF16)
     peers = slots // BLOCK
     is_header = (iota((peers, slots), 1) == iota((peers, slots), 0) * BLOCK + BLOCK - 1).astype(F32).astype(BF16)
-    over_ref[0, 0] = jnp.max(nn(is_header, back[:, :128]))
-
-
-def call(body, outs, args, scratch=(), hbm=(), smem_out=(), flops=0):
+    over_ref[0, 0] = (jnp.max(nn(is_header, back[:, :128])) > 0.0).astype(I32)
+
+
+def call(body, outs, args, scratch=(), hbm=(), smem_out=(), flops=0, mib=8):
     vmem = pl.BlockSpec(memory_space=pltpu.VMEM)
     return pl.pallas_call(
         body,
         out_shape=[jax.ShapeDtypeStruct(shape, kind) for shape, kind in outs],
-        in_specs=[pl.BlockSpec(memory_space=pl.ANY) if i in hbm else vmem for i in range(len(args))],
+        in_specs=[pl.BlockSpec(memory_space=pltpu.HBM) if i in hbm else vmem for i in range(len(args))],
         out_specs=[pl.BlockSpec(memory_space=pltpu.SMEM) if i in smem_out else vmem for i in range(len(outs))],
         scratch_shapes=list(scratch),
         cost_estimate=pl.CostEstimate(flops=flops, transcendentals=0, bytes_accessed=1 << 20),
+        compiler_params=pltpu.CompilerParams(vmem_limit_bytes=mib << 20),
     )(*args)
 
 
@@ -353,6 +354,7 @@
             pltpu.SemaphoreType.DMA((2,)),
         ],
         hbm=(6, 7),
+        mib=60,
         flops=4 * query_rows * tokens * HD,
     )
     got = exchange(send.reshape(peers, BLOCK, width), "batch").reshape(slots, width)
@@ -369,6 +371,7 @@
         cost_estimate=pl.CostEstimate(
             flops=2 * rows * width * heads * output_width, transcendentals=0, bytes_accessed=5 << 20
         ),
+        compiler_params=pltpu.CompilerParams(vmem_limit_bytes=8 << 20),
     )(attention, output_projection_weight)
 
     wide = output_width + HOME_ROWS
@@ -388,7 +391,7 @@
     back = exchange(back.reshape(peers, BLOCK, output_width), "batch").reshape(slots, output_width)
     out, base, over = call(
         tail_kernel,
-        [((rows, output_width), BF16), ((rows, output_width), F32), ((1, 1), F32)],
+        [((rows, output_width), BF16), ((rows, output_width), F32), ((1, 1), I32)],
         [back, parts, target],
         smem_out=(2,),
         flops=2 * rows * slots * output_width,
@@ -400,7 +403,7 @@
         )
         return (base + grown).astype(BF16)
 
-    return lax.cond(over[0, 0] > 0.0, moving, lambda: out)
+    return lax.switch(over[0, 0], [lambda: out, moving])
 
 
 def solution(mesh):

time: 84.5 us -> 77.5 us (0.917)
  Pallas kernels: 20.9 us -> 11.2 us
  waiting for transfers between devices: 10.7 us -> 12.9 us
  local copies, waits for them, and re-layouts: 1.46 us -> 2.83 us
    pallas_call x4, Pallas kernels: 14.4 us -> 9.16 us  [call(): pl.pallas_call(body, out_shape=[jax.ShapeDtypeStruct(shape, kind) for sha...]
    pallas_call x1, Pallas kernels: 6.49 us -> 2.06 us  [per_device(): pl.pallas_call(base_kernel, grid=(heads,), out_shape=jax.ShapeDtypeStruct...]
    all_to_all x1, waiting for transfers between devices: 10.7 us -> 12.9 us  [exchange(): return lax.all_to_all(blocks, axis, split_axis=0, concat_axis=0, tiled=True)]
    unnamed x12 -> x14, local copies, waits for them, and re-layouts: 1.46 us -> 2.83 us
  transfers between devices with their start and end apart: 1 -> 1, of which waited for: 1 -> 1; matrix products, arithmetic and copies ran while one was open for 0% -> 0% of each run, Pallas kernels for 8% -> 3%
where the time goes in v3:
time: 77.5 us; the launch traced here: 77.2 us
  blocking collectives  37.9 us (49%)
  waiting for transfers between devices  12.9 us (17%)
  starting transfers between devices  11.4 us (15%)
  Pallas kernels  11.2 us (14%)
  local copies, waits for them, and re-layouts  2.83 us (4%)
    all_to_all x2, blocking collectives, exchange(): return lax.all_to_all(blocks, axis, split_axis=0, concat_axis=0, tiled=True)  37.9 us
    all_to_all x1, waiting for transfers between devices, exchange(): return lax.all_to_all(blocks, axis, split_axis=0, concat_axis=0, tiled=True)  12.9 us
    all_to_all x1, starting transfers between devices, exchange(): return lax.all_to_all(blocks, axis, split_axis=0, concat_axis=0, tiled=True)  11.4 us
    pallas_call x4, Pallas kernels, call(): pl.pallas_call(body, out_shape=[jax.ShapeDtypeStruct(shape, kind) for sha...  9.16 us
    unnamed x14, local copies, waits for them, and re-layouts  2.83 us
    pallas_call x1, Pallas kernels, per_device(): pl.pallas_call(base_kernel, grid=(heads,), out_shape=jax.ShapeDtypeStruct...  2.06 us
  transfers between devices with their start and end apart: 1, of which 1 were waited for; matrix products, arithmetic and copies ran while one was open for 0% of the time, Pallas kernels for 3%

profile of v3, /device:TPU:32, one launch (start us, length us, event | category | flops | bytes accessed | tf_op | source)
XLA Modules:
  0.0 77.2 jit_solution(16765235146187509547)
XLA Ops:
  0.0 0.0 copy-start.3
  0.0 6.7 %shard_map.111 = (bf16[512,512]{1,0:T(8,128)(2,1)}, bf16[64,512]{1,0:T(8,128)(2,1)S(1)}, s32[1,64]{1,0:T(1,128)}) custom-call(s32[1,512]{1,0:T(1,128)} %index_ref.1, s32[1,64]{1,0:T(1,128)} %count_ref.1, s32[1,64]{1,0:T(1,128)} %bitcast.68, s32[1,64]{1,0:T(1,128)} %bitcast.69, s32[1,32]{1,0:T(1,128)} %list_ref.1, bf16[64,512]{1,0:T(8,128)(2,1)} %q_ref.1, ...), custom_call_target="tpu_custom_call" | custom-call | flops 1073741824 | bytes 1048576 | tf_op jit(solution)/shard_map/pallas_call | solution.py:224
  6.7 11.4 %all-to-all-start.3 = ((bf16[32,16,512]{2,1,0:T(8,128)(2,1)}), bf16[32,16,512]{2,1,0:T(8,128)(2,1)S(1)}, u32[]{:S(2)}, u32[]{:S(2)}) async-start(bf16[32,16,512]{2,1,0:T(8,128)(2,1)} %bitcast.64), calls=%async_computation.3 | async-start | bytes 1048576 | tf_op jit(solution)/shard_map/all_to_all | solution.py:254
  18.1 0.0 copy-start
  18.1 2.2 %copy-done = bf16[512,4096]{1,0:T(8,128)(2,1)S(1)} copy-done((bf16[512,4096]{1,0:T(8,128)(2,1)S(1)}, bf16[512,4096]{1,0:T(8,128)(2,1)}, u32[]{:S(2)}) %copy-start) | copy-done | bytes 4194328
  20.3 0.0 copy-start.2
  20.3 2.1 %shard_map.112.base_ref = bf16[8,64,512]{2,1,0:T(8,128)(2,1)S(1)} custom-call(bf16[64,512]{1,0:T(8,128)(2,1)S(1)} %get-tuple-element.38.attention_ref, bf16[512,4096]{1,0:T(8,128)(2,1)S(1)} %copy-done), custom_call_target="tpu_custom_call" | custom-call | flops 268435456 | bytes 5242880 | tf_op jit(solution)/shard_map/pallas_call | solution.py:362
  22.4 0.0 copy-start.1
  22.4 0.0 copy-start.4
  22.4 0.0 copy-start.5
  22.4 12.9 %all-to-all-done.3 = bf16[32,16,512]{2,1,0:T(8,128)(2,1)S(1)} async-done(((bf16[32,16,512]{2,1,0:T(8,128)(2,1)}), bf16[32,16,512]{2,1,0:T(8,128)(2,1)S(1)}, u32[]{:S(2)}, u32[]{:S(2)}) %all-to-all-start.3) | async-done | bytes 524320 | tf_op jit(solution)/shard_map/all_to_all | solution.py:254
  35.3 0.0 copy-done.3
  35.3 0.9 %shard_map.113 = (bf16[8,64,640]{2,1,0:T(8,128)(2,1)S(1)}, bf16[128,512]{1,0:T(8,128)(2,1)S(1)}, f32[128,128]{1,0:T(8,128)S(1)}, f32[8,128]{1,0:T(8,128)S(1)}) custom-call(bf16[512,512]{1,0:T(8,128)(2,1)S(1)} %bitcast.59, bf16[1024,512]{1,0:T(8,128)(2,1)S(1)} %bitcast.61, bf16[8,64,512]{2,1,0:T(8,128)(2,1)S(1)} %shard_map.112.base_ref), custom_call_target="tpu_custom_call" | custom-call | flops 134217728 | bytes 1048576 | tf_op jit(solution)/shard_map/pallas_call | solution.py:224
  36.2 15.8 %all_to_all.27.parts_ref = bf16[8,64,640]{2,1,0:T(8,128)(2,1)S(1)} all-to-all(bf16[8,64,640]{2,1,0:T(8,128)(2,1)S(1)} %get-tuple-element.39), channel_id=1, replica_groups=mesh['head'=8,'batch'=32] {'head'}, dimensions={0} | all-to-all | bytes 1310720 | tf_op jit(solution)/shard_map/all_to_all | solution.py:254
  52.0 0.0 copy-done.2
  52.0 0.6 shard_map.114
  52.7 22.0 %all_to_all.28 = bf16[32,16,512]{2,1,0:T(8,128)(2,1)S(1)} all-to-all(bf16[32,16,512]{2,1,0:T(8,128)(2,1)S(1)} %bitcast.57), channel_id=1, replica_groups=mesh['head'=8,'batch'=32] {'batch'}, dimensions={0} | all-to-all | bytes 1048576 | tf_op jit(solution)/shard_map/all_to_all | solution.py:254
  74.7 0.0 copy-done.1
  74.7 0.9 %shard_map.115 = (bf16[64,512]{1,0:T(8,128)(2,1)S(1)}, f32[64,512]{1,0:T(8,128)S(1)}, s32[1,1]{1,0:T(1,128)}) custom-call(bf16[512,512]{1,0:T(8,128)(2,1)S(1)} %bitcast.58, bf16[8,64,640]{2,1,0:T(8,128)(2,1)S(1)} %all_to_all.27.parts_ref, s32[1,64]{1,0:T(1,128)S(1)} %copy-done.1), custom_call_target="tpu_custom_call" | custom-call | flops 33554432 | bytes 1048576 | tf_op jit(solution)/shard_map/pallas_call | solution.py:224
  76.3 0.0 copy-done.4
  76.3 0.0 copy-done.5
  76.3 0.2 conditional.1
  76.5 0.0 copy-start.6
  76.6 0.6 copy-done.6
Async XLA Ops:
  0.0 35.3 %copy-start.3 = (bf16[16,512,64]{1,2,0:T(8,128)(2,1)S(1)}, bf16[16,512,64]{1,2,0:T(8,128)(2,1)}, u32[]{:S(2)}) copy-start(bf16[16,512,64]{1,2,0:T(8,128)(2,1)} %param.22) | copy-start | bytes 3145732
  6.7 28.6 %all-to-all-start.3 = ((bf16[32,16,512]{2,1,0:T(8,128)(2,1)}), bf16[32,16,512]{2,1,0:T(8,128)(2,1)S(1)}, u32[]{:S(2)}, u32[]{:S(2)}) async-start(bf16[32,16,512]{2,1,0:T(8,128)(2,1)} %bitcast.64), calls=%async_computation.3 | async-start | bytes 1048576 | tf_op jit(solution)/shard_map/all_to_all | solution.py:254
  18.1 2.2 %copy-start = (bf16[512,4096]{1,0:T(8,128)(2,1)S(1)}, bf16[512,4096]{1,0:T(8,128)(2,1)}, u32[]{:S(2)}) copy-start(bf16[512,4096]{1,0:T(8,128)(2,1)} %weight_ref.1) | copy-start | bytes 12582916
  20.3 31.8 %copy-start.2 = (bf16[16,64,512]{2,1,0:T(8,128)(2,1)S(1)}, bf16[16,64,512]{2,1,0:T(8,128)(2,1)}, u32[]{:S(2)}) copy-start(bf16[16,64,512]{2,1,0:T(8,128)(2,1)} %param.23) | copy-start | bytes 3145732
  22.4 52.4 %copy-start.1 = (s32[1,64]{1,0:T(1,128)S(1)}, s32[1,64]{1,0:T(1,128)}, u32[]{:S(2)}) copy-start(s32[1,64]{1,0:T(1,128)} %get-tuple-element.43.target_ref) | copy-start | bytes 772
  22.4 53.9 %copy-start.4 = (s32[1,32]{1,0:T(1,128)S(1)}, s32[1,32]{1,0:T(1,128)}, u32[]{:S(2)}) copy-start(s32[1,32]{1,0:T(1,128)} %list_ref.1) | copy-start | bytes 388
  22.4 53.9 %copy-start.5 = (s32[64]{0:T(128)S(1)}, s32[64]{0:T(128)}, u32[]{:S(2)}) copy-start(s32[64]{0:T(128)} %param.19) | copy-start | bytes 772
  76.5 0.6 copy-start.6

commit v4 on v3

--- a/solution.py
+++ b/solution.py
@@ -14,6 +14,7 @@
 BLOCK = 16
 HOME_ROWS = 128
 CHUNK = 512
+PIECES = 4
 F32, BF16, I32 = jnp.float32, jnp.bfloat16, jnp.int32
 
 
@@ -35,17 +36,23 @@
 
 
 def source_kernel(
+    index_hbm,
+    count_hbm,
+    last_hbm,
+    entry_hbm,
+    list_hbm,
+    q_hbm,
+    keys_hbm,
+    values_hbm,
+    send_ref,
+    attention_ref,
+    target_ref,
     index_ref,
     count_ref,
     last_ref,
     entry_ref,
     list_ref,
     q_ref,
-    keys_hbm,
-    values_hbm,
-    send_ref,
-    attention_ref,
-    target_ref,
     keys_ref,
     values_ref,
     scores_ref,
@@ -60,10 +67,34 @@
     tokens = pages * PAGE
     groups = HQ // KVH
     steps = tokens // CHUNK
-    copy_keys = pltpu.make_async_copy(keys_hbm, keys_ref, sems.at[0])
-    copy_values = pltpu.make_async_copy(values_hbm, values_ref, sems.at[1])
-    copy_keys.start()
+    piece = tokens // PIECES
+    small = [
+        pltpu.make_async_copy(source, target, sems.at[n])
+        for n, (source, target) in enumerate(
+            [
+                (count_hbm, count_ref),
+                (last_hbm, last_ref),
+                (index_hbm, index_ref),
+                (entry_hbm, entry_ref),
+                (list_hbm, list_ref),
+                (q_hbm, q_ref),
+            ]
+        )
+    ]
+    copy_keys = [
+        pltpu.make_async_copy(
+            keys_hbm.at[pl.ds(n * piece, piece)], keys_ref.at[pl.ds(n * piece, piece)], sems.at[6 + n]
+        )
+        for n in range(PIECES)
+    ]
+    copy_values = pltpu.make_async_copy(values_hbm, values_ref, sems.at[6 + PIECES])
+    for copy in small:
+        copy.start()
+    for copy in copy_keys:
+        copy.start()
     copy_values.start()
+    for copy in small:
+        copy.wait()
 
     count = count_ref[...].astype(F32)
     end = jnp.sum(jnp.where(iota((rows, rows), 1) <= iota((rows, rows), 0), count, 0.0), axis=1, keepdims=True)
@@ -105,9 +136,10 @@
 
     q = jnp.concatenate([q_ref[:, g * HD : (g + 1) * HD] for g in range(groups)], axis=0)
     own = (iota((groups * rows, 128), 0) % rows).astype(F32)
-    copy_keys.wait()
     top = jnp.full((groups * rows, 128), -1e30, F32)
     for step in range(steps):
+        if step * CHUNK % piece == 0:
+            copy_keys[step * CHUNK // piece].wait()
         block = nt(q, keys_ref[step * CHUNK : (step + 1) * CHUNK, :])
         for part in range(CHUNK // 128):
             at = step * (CHUNK // 128) + part
@@ -139,11 +171,16 @@
     send_ref[...] = nn(picked, jnp.concatenate([attention, header], axis=0)).astype(BF16)
 
 
-def base_kernel(attention_ref, weight_ref, out_ref):
-    out_ref[0] = nn(attention_ref[...], weight_ref[...]).astype(BF16)
-
-
-def home_down_kernel(got_ref, down_ref, base_ref, parts_ref, closing_ref, local_ref, over_ref):
+def base_kernel(core_ref, attention_ref, weight_ref, keep_ref, give_ref):
+    half = keep_ref.shape[1]
+    core = core_ref[0, 0]
+    product = nn(attention_ref[...], weight_ref[...])
+    first, second = product[:half], product[half:]
+    keep_ref[0] = jnp.where(core == 0, first, second).astype(BF16)
+    give_ref[0] = jnp.where(core == 0, second, first).astype(BF16)
+
+
+def home_down_kernel(got_ref, down_ref, keep_ref, sibling_ref, parts_ref, closing_ref, local_ref, over_ref):
     slots, width = got_ref.shape
     peers = slots // BLOCK
     got = got_ref[...]
@@ -172,9 +209,12 @@
     for n in range(16):
         total = total + jnp.where(local_lanes == n + 1.0, per_map[n * rank : (n + 1) * rank, :], 0.0)
     total = total.astype(BF16)
-    for h in range(base_ref.shape[0]):
-        parts_ref[h, :, : base_ref.shape[2]] = base_ref[h]
-        parts_ref[h, :, base_ref.shape[2] :] = total
+    heads, half, output_width = keep_ref.shape
+    total = jnp.concatenate([total[:half], total[half:]], axis=1)
+    for h in range(heads):
+        both = keep_ref[h].astype(F32) + sibling_ref[h].astype(F32)
+        parts_ref[h, :, :output_width] = both.astype(BF16)
+        parts_ref[h, :, output_width:] = total
     any_pair = jnp.max(jnp.max(flags, axis=1, keepdims=True), axis=0, keepdims=True)
     served = jnp.sum(filled, axis=0, keepdims=True)
     over = jnp.maximum(any_pair, (served > HOME_ROWS).astype(F32))
@@ -182,18 +222,20 @@
 
 
 def home_up_kernel(parts_ref, up_ref, closing_ref, local_ref, over_ref, back_ref):
-    heads, rank, wide = parts_ref.shape
-    width = wide - HOME_ROWS
+    heads, half, wide = parts_ref.shape
+    rank = 2 * half
+    width = wide - 2 * HOME_ROWS
     slots = closing_ref.shape[1]
     total = parts_ref[0, :, width:].astype(F32)
     for h in range(1, heads):
         total = total + parts_ref[h, :, width:].astype(F32)
+    total = jnp.concatenate([total[:, :HOME_ROWS], total[:, HOME_ROWS:]], axis=0)
     ranked = jnp.concatenate([total, total], axis=0).T
     local = local_ref[...]
     stored = up_ref.shape[0] // rank
-    half = iota((HOME_ROWS, 128), 1) // rank
+    side = iota((HOME_ROWS, 128), 1) // rank
     spread = jnp.concatenate(
-        [jnp.where(local == (half + 2 * pair + 1).astype(F32), ranked, 0.0).astype(BF16) for pair in range(stored // 2)],
+        [jnp.where(local == (side + 2 * pair + 1).astype(F32), ranked, 0.0).astype(BF16) for pair in range(stored // 2)],
         axis=1,
     )
     grown = nn(spread, up_ref[...]).astype(BF16)
@@ -204,11 +246,13 @@
 
 
 def tail_kernel(back_ref, parts_ref, target_ref, out_ref, base_ref, over_ref):
-    heads, rows, wide = parts_ref.shape
+    heads, half, wide = parts_ref.shape
+    rows = 2 * half
     slots, width = back_ref.shape
-    base = parts_ref[0, :, :width].astype(F32)
-    for h in range(1, heads):
-        base = base + parts_ref[h, :, :width].astype(F32)
+    base = [parts_ref[core, :, :width].astype(F32) for core in range(2)]
+    for h in range(2, heads):
+        base[h % 2] = base[h % 2] + parts_ref[h, :, :width].astype(F32)
+    base = jnp.concatenate(base, axis=0)
     base_ref[...] = base
     target = column(target_ref[...].astype(F32))
     picked = (iota((rows, slots), 1).astype(F32) == target).astype(F32).astype(BF16)
@@ -347,38 +391,49 @@
             value_page_cache.reshape(tokens, HD),
         ],
         scratch=[
+            pltpu.VMEM((1, pages), I32),
+            pltpu.VMEM((1, rows), I32),
+            pltpu.VMEM((1, rows), I32),
+            pltpu.VMEM((1, rows), I32),
+            pltpu.VMEM((1, batch_adapters.shape[1]), I32),
+            pltpu.VMEM((rows, width), BF16),
             pltpu.VMEM((tokens, HD), BF16),
             pltpu.VMEM((tokens, HD), BF16),
             pltpu.VMEM((query_rows, tokens), F32),
             pltpu.VMEM((tokens // 128, 128), F32),
-            pltpu.SemaphoreType.DMA((2,)),
+            pltpu.SemaphoreType.DMA((7 + PIECES,)),
         ],
-        hbm=(6, 7),
+        hbm=range(8),
         mib=60,
         flops=4 * query_rows * tokens * HD,
     )
     got = exchange(send.reshape(peers, BLOCK, width), "batch").reshape(slots, width)
 
-    base = pl.pallas_call(
+    half = rows // 2
+    core = (lax.axis_index("head") & 1).astype(I32).reshape(1, 1)
+    base_block = pl.BlockSpec((1, half, output_width), lambda h: (h, 0, 0))
+    keep, give = pl.pallas_call(
         base_kernel,
         grid=(heads,),
-        out_shape=jax.ShapeDtypeStruct((heads, rows, output_width), BF16),
+        out_shape=[jax.ShapeDtypeStruct((heads, half, output_width), BF16)] * 2,
         in_specs=[
+            pl.BlockSpec(memory_space=pltpu.SMEM),
             pl.BlockSpec((rows, width), lambda h: (0, 0)),
             pl.BlockSpec((width, output_width), lambda h: (0, h)),
         ],
-        out_specs=pl.BlockSpec((1, rows, output_width), lambda h: (h, 0, 0)),
+        out_specs=[base_block, base_block],
         cost_estimate=pl.CostEstimate(
             flops=2 * rows * width * heads * output_width, transcendentals=0, bytes_accessed=5 << 20
         ),
         compiler_params=pltpu.CompilerParams(vmem_limit_bytes=8 << 20),
-    )(attention, output_projection_weight)
-
-    wide = output_width + HOME_ROWS
+    )(core, attention, output_projection_weight)
+    sibling = lax.ppermute(give, "head", [(h, h ^ 1) for h in range(heads)])
+
+    wide = output_width + 2 * HOME_ROWS
     parts, closing, local, over = call(
         home_down_kernel,
-        [((heads, rank, wide), BF16), ((HOME_ROWS, slots), BF16), ((HOME_ROWS, HOME_ROWS), F32), ((8, 128), F32)],
-        [got, jnp.swapaxes(adapter_down_weight, 1, 2).reshape(stored * rank, width), base],
+        [((heads, half, wide), BF16), ((HOME_ROWS, slots), BF16), ((HOME_ROWS, HOME_ROWS), F32), ((8, 128), F32)],
+        [got, jnp.swapaxes(adapter_down_weight, 1, 2).reshape(stored * rank, width), keep, sibling],
         flops=2 * HOME_ROWS * width * stored * rank,
     )
     parts = exchange(parts, "head")

time: 77.5 us -> 74.2 us (0.957)
  blocking collectives: 37.9 us -> 35 us
    all_to_all x2, blocking collectives: 37.9 us -> 35 us  [exchange(): return lax.all_to_all(blocks, axis, split_axis=0, concat_axis=0, tiled=True)]
    all_to_all x1, waiting for transfers between devices: 12.9 us -> 11.2 us  [exchange(): return lax.all_to_all(blocks, axis, split_axis=0, concat_axis=0, tiled=True)]
    ppermute x0 -> x1, waiting for transfers between devices: none -> 1.52 us  [per_device(): sibling = lax.ppermute(give, 'head', [(h, h ^ 1) for h in range(heads)])]
  transfers between devices with their start and end apart: 1 -> 2, of which waited for: 1 -> 2; matrix products, arithmetic and copies ran while one was open for 0% -> 0% of each run, Pallas kernels for 3% -> 3%
where the time goes in v4:
time: 74.2 us; the launch traced here: 73.9 us
  blocking collectives  35 us (47%)
  waiting for transfers between devices  12.8 us (17%)
  starting transfers between devices  11.6 us (16%)
  Pallas kernels  10.7 us (14%)
  local copies, waits for them, and re-layouts  2.83 us (4%)
  between operations  0.78 us (1%)
    all_to_all x2, blocking collectives, exchange(): return lax.all_to_all(blocks, axis, split_axis=0, concat_axis=0, tiled=True)  35 us
    all_to_all x1, starting transfers between devices, exchange(): return lax.all_to_all(blocks, axis, split_axis=0, concat_axis=0, tiled=True)  11.5 us
    all_to_all x1, waiting for transfers between devices, exchange(): return lax.all_to_all(blocks, axis, split_axis=0, concat_axis=0, tiled=True)  11.2 us
    pallas_call x4, Pallas kernels, call(): pl.pallas_call(body, out_shape=[jax.ShapeDtypeStruct(shape, kind) for sha...  8.56 us
    unnamed x14, local copies, waits for them, and re-layouts  2.83 us
    pallas_call x1, Pallas kernels, per_device(): pl.pallas_call(base_kernel, grid=(heads,), out_shape=[jax.ShapeDtypeStruc...  2.1 us
    ppermute x1, waiting for transfers between devices, per_device(): sibling = lax.ppermute(give, 'head', [(h, h ^ 1) for h in range(heads)])  1.52 us
  transfers between devices with their start and end apart: 2, of which 2 were waited for; matrix products, arithmetic and copies ran while one was open for 0% of the time, Pallas kernels for 3%

profile of v4, /device:TPU:32, one launch (start us, length us, event | category | flops | bytes accessed | tf_op | source)
XLA Modules:
  0.0 73.9 jit_solution(11038601079903630742)
XLA Ops:
  0.0 6.1 %shard_map.111 = (bf16[512,512]{1,0:T(8,128)(2,1)}, bf16[64,512]{1,0:T(8,128)(2,1)S(1)}, s32[1,64]{1,0:T(1,128)}) custom-call(s32[1,512]{1,0:T(1,128)} %index_hbm.1, s32[1,64]{1,0:T(1,128)} %count_hbm.1, s32[1,64]{1,0:T(1,128)} %bitcast.69, s32[1,64]{1,0:T(1,128)} %bitcast.70, s32[1,32]{1,0:T(1,128)} %list_hbm.1, bf16[64,512]{1,0:T(8,128)(2,1)} %q_hbm.1, ...), custom_call_target="tpu_custom_call" | custom-call | flops 1073741824 | bytes 1048576 | tf_op jit(solution)/shard_map/pallas_call | solution.py:268
  6.1 0.0 copy-start.3
  6.1 11.5 %all-to-all-start.3 = ((bf16[32,16,512]{2,1,0:T(8,128)(2,1)}), bf16[32,16,512]{2,1,0:T(8,128)(2,1)S(1)}, u32[]{:S(2)}, u32[]{:S(2)}) async-start(bf16[32,16,512]{2,1,0:T(8,128)(2,1)} %bitcast.65), calls=%async_computation.3 | async-start | bytes 1048576 | tf_op jit(solution)/shard_map/all_to_all | solution.py:298
  17.7 0.0 copy-start
  17.7 2.2 %copy-done = bf16[512,4096]{1,0:T(8,128)(2,1)S(1)} copy-done((bf16[512,4096]{1,0:T(8,128)(2,1)S(1)}, bf16[512,4096]{1,0:T(8,128)(2,1)}, u32[]{:S(2)}) %copy-start) | copy-done | bytes 4194328
  19.8 2.1 %shard_map.112 = (bf16[8,32,512]{2,1,0:T(8,128)(2,1)S(1)}, bf16[8,32,512]{2,1,0:T(8,128)(2,1)S(1)}) custom-call(s32[1,1]{1,0:T(1,128)} %bitcast.28.core_ref, bf16[64,512]{1,0:T(8,128)(2,1)S(1)} %get-tuple-element.40.attention_ref, bf16[512,4096]{1,0:T(8,128)(2,1)S(1)} %copy-done), custom_call_target="tpu_custom_call" | custom-call | flops 268435456 | bytes 5242880 | tf_op jit(solution)/shard_map/pallas_call | solution.py:415
  22.0 0.0 copy-start.4
  22.0 0.0 copy-start.5
  22.0 0.1 collective-permute-start
  22.1 1.5 %collective-permute-done.sibling_ref = bf16[8,32,512]{2,1,0:T(8,128)(2,1)S(1)} collective-permute-done((bf16[8,32,512]{2,1,0:T(8,128)(2,1)S(1)}, bf16[8,32,512]{2,1,0:T(8,128)(2,1)S(1)}, u32[]{:S(2)}, u32[]{:S(2)}) %collective-permute-start) | collective-permute-done | bytes 262176 | tf_op jit(solution)/shard_map/ppermute | solution.py:430
  23.6 11.2 %all-to-all-done.3 = bf16[32,16,512]{2,1,0:T(8,128)(2,1)S(1)} async-done(((bf16[32,16,512]{2,1,0:T(8,128)(2,1)}), bf16[32,16,512]{2,1,0:T(8,128)(2,1)S(1)}, u32[]{:S(2)}, u32[]{:S(2)}) %all-to-all-start.3) | async-done | bytes 524320 | tf_op jit(solution)/shard_map/all_to_all | solution.py:298
  34.8 0.0 copy-done.2
  34.8 0.9 %shard_map.113 = (bf16[8,32,768]{2,1,0:T(8,128)(2,1)S(1)}, bf16[128,512]{1,0:T(8,128)(2,1)S(1)}, f32[128,128]{1,0:T(8,128)S(1)}, f32[8,128]{1,0:T(8,128)S(1)}) custom-call(bf16[512,512]{1,0:T(8,128)(2,1)S(1)} %bitcast.59, bf16[1024,512]{1,0:T(8,128)(2,1)S(1)} %bitcast.61, bf16[8,32,512]{2,1,0:T(8,128)(2,1)S(1)} %get-tuple-element.41.keep_ref, ...), custom_call_target="tpu_custom_call" | custom-call | flops 134217728 | bytes 1048576 | tf_op jit(solution)/shard_map/pallas_call | solution.py:268
  35.7 13.0 %all_to_all.27.parts_ref = bf16[8,32,768]{2,1,0:T(8,128)(2,1)S(1)} all-to-all(bf16[8,32,768]{2,1,0:T(8,128)(2,1)S(1)} %get-tuple-element.43), channel_id=1, replica_groups=mesh['head'=8,'batch'=32] {'head'}, dimensions={0} | all-to-all | bytes 786432 | tf_op jit(solution)/shard_map/all_to_all | solution.py:298
  48.8 0.0 copy-done.3
  48.8 0.6 shard_map.114
  49.4 22.0 %all_to_all.28 = bf16[32,16,512]{2,1,0:T(8,128)(2,1)S(1)} all-to-all(bf16[32,16,512]{2,1,0:T(8,128)(2,1)S(1)} %bitcast.60), channel_id=1, replica_groups=mesh['head'=8,'batch'=32] {'batch'}, dimensions={0} | all-to-all | bytes 1048576 | tf_op jit(solution)/shard_map/all_to_all | solution.py:298
  71.4 0.0 copy-done.1
  71.4 0.9 %shard_map.115 = (bf16[64,512]{1,0:T(8,128)(2,1)S(1)}, f32[64,512]{1,0:T(8,128)S(1)}, s32[1,1]{1,0:T(1,128)}) custom-call(bf16[512,512]{1,0:T(8,128)(2,1)S(1)} %bitcast.58, bf16[8,32,768]{2,1,0:T(8,128)(2,1)S(1)} %all_to_all.27.parts_ref, s32[1,64]{1,0:T(1,128)S(1)} %copy-done.1), custom_call_target="tpu_custom_call" | custom-call | flops 33554432 | bytes 1048576 | tf_op jit(solution)/shard_map/pallas_call | solution.py:268
  73.0 0.0 copy-done.4
  73.0 0.0 copy-done.5
  73.0 0.2 conditional.1
  73.3 0.0 copy-start.6
  73.3 0.6 copy-done.6
  (2 shorter events, 0.0 us)
Async XLA Ops:
  0.0 34.8 %copy-start.2 = (bf16[16,512,64]{1,2,0:T(8,128)(2,1)S(1)}, bf16[16,512,64]{1,2,0:T(8,128)(2,1)}, u32[]{:S(2)}) copy-start(bf16[16,512,64]{1,2,0:T(8,128)(2,1)} %param.22) | copy-start | bytes 3145732
  6.1 42.6 %copy-start.3 = (bf16[16,64,512]{2,1,0:T(8,128)(2,1)S(1)}, bf16[16,64,512]{2,1,0:T(8,128)(2,1)}, u32[]{:S(2)}) copy-start(bf16[16,64,512]{2,1,0:T(8,128)(2,1)} %param.23) | copy-start | bytes 3145732
  6.1 28.7 %all-to-all-start.3 = ((bf16[32,16,512]{2,1,0:T(8,128)(2,1)}), bf16[32,16,512]{2,1,0:T(8,128)(2,1)S(1)}, u32[]{:S(2)}, u32[]{:S(2)}) async-start(bf16[32,16,512]{2,1,0:T(8,128)(2,1)} %bitcast.65), calls=%async_computation.3 | async-start | bytes 1048576 | tf_op jit(solution)/shard_map/all_to_all | solution.py:298
  17.7 2.2 %copy-start = (bf16[512,4096]{1,0:T(8,128)(2,1)S(1)}, bf16[512,4096]{1,0:T(8,128)(2,1)}, u32[]{:S(2)}) copy-start(bf16[512,4096]{1,0:T(8,128)(2,1)} %weight_ref.1) | copy-start | bytes 12582916
  19.8 51.6 %copy-start.1 = (s32[1,64]{1,0:T(1,128)S(1)}, s32[1,64]{1,0:T(1,128)}, u32[]{:S(2)}) copy-start(s32[1,64]{1,0:T(1,128)} %get-tuple-element.47.target_ref) | copy-start | bytes 772
  22.0 51.1 %copy-start.4 = (s32[1,32]{1,0:T(1,128)S(1)}, s32[1,32]{1,0:T(1,128)}, u32[]{:S(2)}) copy-start(s32[1,32]{1,0:T(1,128)} %list_hbm.1) | copy-start | bytes 388
  22.0 51.0 %copy-start.5 = (s32[64]{0:T(128)S(1)}, s32[64]{0:T(128)}, u32[]{:S(2)}) copy-start(s32[64]{0:T(128)} %param.19) | copy-start | bytes 772
  22.0 1.6 %collective-permute-start = (bf16[8,32,512]{2,1,0:T(8,128)(2,1)S(1)}, bf16[8,32,512]{2,1,0:T(8,128)(2,1)S(1)}, u32[]{:S(2)}, u32[]{:S(2)}) collective-permute-start(bf16[8,32,512]{2,1,0:T(8,128)(2,1)S(1)} %get-tuple-element.42), channel_id=1, source_target_pairs={{0,32},{32,0},{64,96},{96,64},{128,160},{160,128},{192,224},{224,1... | collective-permute-start | bytes 786440 | tf_op jit(solution)/shard_map/ppermute | solution.py:430
  73.3 0.6 copy-start.6

commit v5 on v4

--- a/solution.py
+++ b/solution.py
@@ -171,16 +171,26 @@
     send_ref[...] = nn(picked, jnp.concatenate([attention, header], axis=0)).astype(BF16)
 
 
-def base_kernel(core_ref, attention_ref, weight_ref, keep_ref, give_ref):
-    half = keep_ref.shape[1]
-    core = core_ref[0, 0]
-    product = nn(attention_ref[...], weight_ref[...])
-    first, second = product[:half], product[half:]
-    keep_ref[0] = jnp.where(core == 0, first, second).astype(BF16)
-    give_ref[0] = jnp.where(core == 0, second, first).astype(BF16)
-
-
-def home_down_kernel(got_ref, down_ref, keep_ref, sibling_ref, parts_ref, closing_ref, local_ref, over_ref):
+def base_kernel(place_ref, attention_ref, weight_ref, keep_ref, give_ref):
+    heads, half, output_width = keep_ref.shape
+    first = place_ref[0, 0] == 0
+    attention = attention_ref[...]
+    for h in range(heads):
+        product = nn(attention, weight_ref[:, h * output_width : (h + 1) * output_width])
+        keep_ref[h] = jnp.where(first, product[:half], product[half:]).astype(BF16)
+        give_ref[h] = jnp.where(first, product[half:], product[:half]).astype(BF16)
+
+
+def pair_kernel(place_ref, keep_ref, sibling_ref, keep_out_ref, give_out_ref):
+    heads, quarter, _ = keep_out_ref.shape
+    first = place_ref[0, 1] == 0
+    for h in range(heads):
+        both = keep_ref[h].astype(F32) + sibling_ref[h].astype(F32)
+        keep_out_ref[h] = jnp.where(first, both[:quarter], both[quarter:]).astype(BF16)
+        give_out_ref[h] = jnp.where(first, both[quarter:], both[:quarter]).astype(BF16)
+
+
+def home_down_kernel(got_ref, down_ref, keep_ref, other_ref, parts_ref, closing_ref, local_ref, over_ref):
     slots, width = got_ref.shape
     peers = slots // BLOCK
     got = got_ref[...]
@@ -209,10 +219,10 @@
     for n in range(16):
         total = total + jnp.where(local_lanes == n + 1.0, per_map[n * rank : (n + 1) * rank, :], 0.0)
     total = total.astype(BF16)
-    heads, half, output_width = keep_ref.shape
-    total = jnp.concatenate([total[:half], total[half:]], axis=1)
+    heads, quarter, output_width = keep_ref.shape
+    total = jnp.concatenate([total[n * quarter : (n + 1) * quarter] for n in range(4)], axis=1)
     for h in range(heads):
-        both = keep_ref[h].astype(F32) + sibling_ref[h].astype(F32)
+        both = keep_ref[h].astype(F32) + other_ref[h].astype(F32)
         parts_ref[h, :, :output_width] = both.astype(BF16)
         parts_ref[h, :, output_width:] = total
     any_pair = jnp.max(jnp.max(flags, axis=1, keepdims=True), axis=0, keepdims=True)
@@ -222,14 +232,14 @@
 
 
 def home_up_kernel(parts_ref, up_ref, closing_ref, local_ref, over_ref, back_ref):
-    heads, half, wide = parts_ref.shape
-    rank = 2 * half
-    width = wide - 2 * HOME_ROWS
+    heads, quarter, wide = parts_ref.shape
+    rank = 4 * quarter
+    width = wide - 4 * HOME_ROWS
     slots = closing_ref.shape[1]
     total = parts_ref[0, :, width:].astype(F32)
     for h in range(1, heads):
         total = total + parts_ref[h, :, width:].astype(F32)
-    total = jnp.concatenate([total[:, :HOME_ROWS], total[:, HOME_ROWS:]], axis=0)
+    total = jnp.concatenate([total[:, n * HOME_ROWS : (n + 1) * HOME_ROWS] for n in range(4)], axis=0)
     ranked = jnp.concatenate([total, total], axis=0).T
     local = local_ref[...]
     stored = up_ref.shape[0] // rank
@@ -246,30 +256,35 @@
 
 
 def tail_kernel(back_ref, parts_ref, target_ref, out_ref, base_ref, over_ref):
-    heads, half, wide = parts_ref.shape
-    rows = 2 * half
+    heads = parts_ref.shape[0]
+    rows = target_ref.shape[1]
     slots, width = back_ref.shape
-    base = [parts_ref[core, :, :width].astype(F32) for core in range(2)]
-    for h in range(2, heads):
-        base[h % 2] = base[h % 2] + parts_ref[h, :, :width].astype(F32)
+    base = [
+        parts_ref[2 * side + core, :, :width].astype(F32) + parts_ref[heads // 2 + 2 * side + core, :, :width].astype(F32)
+        for core in range(2)
+        for side in range(2)
+    ]
     base = jnp.concatenate(base, axis=0)
-    base_ref[...] = base
     target = column(target_ref[...].astype(F32))
     picked = (iota((rows, slots), 1).astype(F32) == target).astype(F32).astype(BF16)
     back = back_ref[...]
     out_ref[...] = (base + nn(picked, back)).astype(BF16)
+    base_ref[...] = base
     peers = slots // BLOCK
     is_header = (iota((peers, slots), 1) == iota((peers, slots), 0) * BLOCK + BLOCK - 1).astype(F32).astype(BF16)
     over_ref[0, 0] = (jnp.max(nn(is_header, back[:, :128])) > 0.0).astype(I32)
 
 
-def call(body, outs, args, scratch=(), hbm=(), smem_out=(), flops=0, mib=8):
-    vmem = pl.BlockSpec(memory_space=pltpu.VMEM)
+def call(body, outs, args, scratch=(), hbm=(), smem=(), smem_out=(), flops=0, mib=8):
+    def spec(n, in_hbm, in_smem):
+        space = pltpu.HBM if n in in_hbm else pltpu.SMEM if n in in_smem else pltpu.VMEM
+        return pl.BlockSpec(memory_space=space)
+
     return pl.pallas_call(
         body,
         out_shape=[jax.ShapeDtypeStruct(shape, kind) for shape, kind in outs],
-        in_specs=[pl.BlockSpec(memory_space=pltpu.HBM) if i in hbm else vmem for i in range(len(args))],
-        out_specs=[pl.BlockSpec(memory_space=pltpu.SMEM) if i in smem_out else vmem for i in range(len(outs))],
+        in_specs=[spec(n, hbm, smem) for n in range(len(args))],
+        out_specs=[spec(n, (), smem_out) for n in range(len(outs))],
         scratch_shapes=list(scratch),
         cost_estimate=pl.CostEstimate(flops=flops, transcendentals=0, bytes_accessed=1 << 20),
         compiler_params=pltpu.CompilerParams(vmem_limit_bytes=mib << 20),
@@ -409,31 +424,28 @@
     )
     got = exchange(send.reshape(peers, BLOCK, width), "batch").reshape(slots, width)
 
-    half = rows // 2
-    core = (lax.axis_index("head") & 1).astype(I32).reshape(1, 1)
-    base_block = pl.BlockSpec((1, half, output_width), lambda h: (h, 0, 0))
-    keep, give = pl.pallas_call(
+    half, quarter = rows // 2, rows // 4
+    head = lax.axis_index("head").astype(I32)
+    place = jnp.stack([head & 1, (head >> 1) & 1]).reshape(1, 2)
+    keep, give = call(
         base_kernel,
-        grid=(heads,),
-        out_shape=[jax.ShapeDtypeStruct((heads, half, output_width), BF16)] * 2,
-        in_specs=[
-            pl.BlockSpec(memory_space=pltpu.SMEM),
-            pl.BlockSpec((rows, width), lambda h: (0, 0)),
-            pl.BlockSpec((width, output_width), lambda h: (0, h)),
-        ],
-        out_specs=[base_block, base_block],
-        cost_estimate=pl.CostEstimate(
-            flops=2 * rows * width * heads * output_width, transcendentals=0, bytes_accessed=5 << 20
-        ),
-        compiler_params=pltpu.CompilerParams(vmem_limit_bytes=8 << 20),
-    )(core, attention, output_projection_weight)
+        [((heads, half, output_width), BF16)] * 2,
+        [place, attention, output_projection_weight],
+        smem=(0,),
+        flops=2 * rows * width * heads * output_width,
+        mib=12,
+    )
     sibling = lax.ppermute(give, "head", [(h, h ^ 1) for h in range(heads)])
-
-    wide = output_width + 2 * HOME_ROWS
+    keep, give = call(
+        pair_kernel, [((heads, quarter, output_width), BF16)] * 2, [place, keep, sibling], smem=(0,), flops=1 << 20
+    )
+    other = lax.ppermute(give, "head", [(h, h ^ 2) for h in range(heads)])
+
+    wide = output_width + 4 * HOME_ROWS
     parts, closing, local, over = call(
         home_down_kernel,
-        [((heads, half, wide), BF16), ((HOME_ROWS, slots), BF16), ((HOME_ROWS, HOME_ROWS), F32), ((8, 128), F32)],
-        [got, jnp.swapaxes(adapter_down_weight, 1, 2).reshape(stored * rank, width), keep, sibling],
+        [((heads, quarter, wide), BF16), ((HOME_ROWS, slots), BF16), ((HOME_ROWS, HOME_ROWS), F32), ((8, 128), F32)],
+        [got, jnp.swapaxes(adapter_down_weight, 1, 2).reshape(stored * rank, width), keep, other],
         flops=2 * HOME_ROWS * width * stored * rank,
     )
     parts = exchange(parts, "head")

time: 74.2 us -> 72.6 us (0.978)
  blocking collectives: 35 us -> 33.4 us
  waiting for transfers between devices: 12.8 us -> 11.2 us
  starting transfers between devices: 11.6 us -> 13.2 us
    all_to_all x1, waiting for transfers between devices: 11.2 us -> 5.63 us  [exchange(): return lax.all_to_all(blocks, axis, split_axis=0, concat_axis=0, tiled=True)]
    ppermute x0 -> x1, waiting for transfers between devices: none -> 4.05 us  [per_device(): other = lax.ppermute(give, 'head', [(h, h ^ 2) for h in range(heads)])]
    pallas_call x1 -> x0, Pallas kernels: 2.1 us -> none  [per_device(): pl.pallas_call(base_kernel, grid=(heads,), out_shape=[jax.ShapeDtypeStruc...]
    pallas_call x4 -> x6, Pallas kernels: 8.56 us -> 10.6 us  [call(): pl.pallas_call(body, out_shape=[jax.ShapeDtypeStruct(shape, kind) for sha...]
    all_to_all x2, blocking collectives: 35 us -> 33.4 us  [exchange(): return lax.all_to_all(blocks, axis, split_axis=0, concat_axis=0, tiled=True)]
    ppermute x0 -> x1, starting transfers between devices: none -> 1.58 us  [per_device(): other = lax.ppermute(give, 'head', [(h, h ^ 2) for h in range(heads)])]
  transfers between devices with their start and end apart: 2 -> 3, of which waited for: 2 -> 3; matrix products, arithmetic and copies ran while one was open for 0% -> 0% of each run, Pallas kernels for 3% -> 3%
where the time goes in v5:
time: 72.6 us; the launch traced here: 72.3 us
  blocking collectives  33.4 us (46%)
  starting transfers between devices  13.2 us (18%)
  waiting for transfers between devices  11.2 us (15%)
  Pallas kernels  10.6 us (15%)
  local copies, waits for them, and re-layouts  2.84 us (4%)
  between operations  0.78 us (1%)
    all_to_all x2, blocking collectives, exchange(): return lax.all_to_all(blocks, axis, split_axis=0, concat_axis=0, tiled=True)  33.4 us
    all_to_all x1, starting transfers between devices, exchange(): return lax.all_to_all(blocks, axis, split_axis=0, concat_axis=0, tiled=True)  11.5 us
    pallas_call x6, Pallas kernels, call(): pl.pallas_call(body, out_shape=[jax.ShapeDtypeStruct(shape, kind) for sha...  10.6 us
    all_to_all x1, waiting for transfers between devices, exchange(): return lax.all_to_all(blocks, axis, split_axis=0, concat_axis=0, tiled=True)  5.63 us
    ppermute x1, waiting for transfers between devices, per_device(): other = lax.ppermute(give, 'head', [(h, h ^ 2) for h in range(heads)])  4.05 us
    unnamed x14, local copies, waits for them, and re-layouts  2.84 us
    ppermute x1, starting transfers between devices, per_device(): other = lax.ppermute(give, 'head', [(h, h ^ 2) for h in range(heads)])  1.58 us
    ppermute x1, waiting for transfers between devices, per_device(): sibling = lax.ppermute(give, 'head', [(h, h ^ 1) for h in range(heads)])  1.52 us
  transfers between devices with their start and end apart: 3, of which 3 were waited for; matrix products, arithmetic and copies ran while one was open for 0% of the time, Pallas kernels for 3%

profile of v5, /device:TPU:32, one launch (start us, length us, event | category | flops | bytes accessed | tf_op | source)
XLA Modules:
  0.0 72.3 jit_solution(10662002830228578966)
XLA Ops:
  0.0 6.1 %shard_map.111 = (bf16[512,512]{1,0:T(8,128)(2,1)}, bf16[64,512]{1,0:T(8,128)(2,1)S(1)}, s32[1,64]{1,0:T(1,128)}) custom-call(s32[1,512]{1,0:T(1,128)} %index_hbm.1, s32[1,64]{1,0:T(1,128)} %count_hbm.1, s32[1,64]{1,0:T(1,128)} %bitcast.72, s32[1,64]{1,0:T(1,128)} %bitcast.73, s32[1,32]{1,0:T(1,128)} %list_hbm.1, bf16[64,512]{1,0:T(8,128)(2,1)} %q_hbm.1, ...), custom_call_target="tpu_custom_call" | custom-call | flops 1073741824 | bytes 1048576 | tf_op jit(solution)/shard_map/pallas_call | solution.py:283
  6.1 0.0 copy-start.3
  6.1 11.5 %all-to-all-start.3 = ((bf16[32,16,512]{2,1,0:T(8,128)(2,1)}), bf16[32,16,512]{2,1,0:T(8,128)(2,1)S(1)}, u32[]{:S(2)}, u32[]{:S(2)}) async-start(bf16[32,16,512]{2,1,0:T(8,128)(2,1)} %bitcast.68), calls=%async_computation.3 | async-start | bytes 1048576 | tf_op jit(solution)/shard_map/all_to_all | solution.py:313
  17.7 0.1 add_bitcast_fusion.place_ref
  17.7 2.2 %copy-done = bf16[512,4096]{1,0:T(8,128)(2,1)S(1)} copy-done((bf16[512,4096]{1,0:T(8,128)(2,1)S(1)}, bf16[512,4096]{1,0:T(8,128)(2,1)}, u32[]{:S(2)}) %copy-start) | copy-done | bytes 4194328
  19.9 1.4 %shard_map.112 = (bf16[8,32,512]{2,1,0:T(8,128)(2,1)S(1)}, bf16[8,32,512]{2,1,0:T(8,128)(2,1)S(1)}) custom-call(s32[1,2]{1,0:T(1,128)S(1)} %add_bitcast_fusion.place_ref, bf16[64,512]{1,0:T(8,128)(2,1)S(1)} %get-tuple-element.42.attention_ref, bf16[512,4096]{1,0:T(8,128)(2,1)S(1)} %copy-done), custom_call_target="tpu_custom_call" | custom-call | flops 268435456 | bytes 1048576 | tf_op jit(solution)/shard_map/pallas_call | solution.py:283
  21.3 0.0 copy-start.4
  21.3 0.0 copy-start.5
  21.3 0.1 collective-permute-start
  21.4 1.5 %collective-permute-done.sibling_ref = bf16[8,32,512]{2,1,0:T(8,128)(2,1)S(1)} collective-permute-done((bf16[8,32,512]{2,1,0:T(8,128)(2,1)S(1)}, bf16[8,32,512]{2,1,0:T(8,128)(2,1)S(1)}, u32[]{:S(2)}, u32[]{:S(2)}) %collective-permute-start) | collective-permute-done | bytes 262176 | tf_op jit(solution)/shard_map/ppermute | solution.py:438
  22.9 0.6 shard_map.113
  23.6 1.6 %collective-permute-start.1 = (bf16[8,16,512]{2,1,0:T(8,128)(2,1)S(1)}, bf16[8,16,512]{2,1,0:T(8,128)(2,1)S(1)}, u32[]{:S(2)}, u32[]{:S(2)}) collective-permute-start(bf16[8,16,512]{2,1,0:T(8,128)(2,1)S(1)} %get-tuple-element.46), channel_id=1, source_target_pairs={{0,64},{32,96},{64,0},{96,32},{128,192},{160,224},{192,128},{224,1... | collective-permute-start | bytes 393224 | tf_op jit(solution)/shard_map/ppermute | solution.py:442
  25.2 4.0 %collective-permute-done.1.other_ref = bf16[8,16,512]{2,1,0:T(8,128)(2,1)S(1)} collective-permute-done((bf16[8,16,512]{2,1,0:T(8,128)(2,1)S(1)}, bf16[8,16,512]{2,1,0:T(8,128)(2,1)S(1)}, u32[]{:S(2)}, u32[]{:S(2)}) %collective-permute-start.1) | collective-permute-done | bytes 131104 | tf_op jit(solution)/shard_map/ppermute | solution.py:442
  29.2 5.6 %all-to-all-done.3 = bf16[32,16,512]{2,1,0:T(8,128)(2,1)S(1)} async-done(((bf16[32,16,512]{2,1,0:T(8,128)(2,1)}), bf16[32,16,512]{2,1,0:T(8,128)(2,1)S(1)}, u32[]{:S(2)}, u32[]{:S(2)}) %all-to-all-start.3) | async-done | bytes 524320 | tf_op jit(solution)/shard_map/all_to_all | solution.py:313
  34.8 0.0 copy-done.2
  34.8 0.9 %shard_map.114 = (bf16[8,16,1024]{2,1,0:T(8,128)(2,1)S(1)}, bf16[128,512]{1,0:T(8,128)(2,1)S(1)}, f32[128,128]{1,0:T(8,128)S(1)}, f32[8,128]{1,0:T(8,128)S(1)}) custom-call(bf16[512,512]{1,0:T(8,128)(2,1)S(1)} %bitcast.61, bf16[1024,512]{1,0:T(8,128)(2,1)S(1)} %bitcast.64, bf16[8,16,512]{2,1,0:T(8,128)(2,1)S(1)} %get-tuple-element.45.keep_ref, ...), custom_call_target="tpu_custom_call" | custom-call | flops 134217728 | bytes 1048576 | tf_op jit(solution)/shard_map/pallas_call | solution.py:283
  35.8 11.6 %all_to_all.27.parts_ref = bf16[8,16,1024]{2,1,0:T(8,128)(2,1)S(1)} all-to-all(bf16[8,16,1024]{2,1,0:T(8,128)(2,1)S(1)} %get-tuple-element.47), channel_id=1, replica_groups=mesh['head'=8,'batch'=32] {'head'}, dimensions={0} | all-to-all | bytes 524288 | tf_op jit(solution)/shard_map/all_to_all | solution.py:313
  47.4 0.0 copy-done.3
  47.4 0.6 shard_map.115
  48.0 21.8 %all_to_all.28 = bf16[32,16,512]{2,1,0:T(8,128)(2,1)S(1)} all-to-all(bf16[32,16,512]{2,1,0:T(8,128)(2,1)S(1)} %bitcast.63), channel_id=1, replica_groups=mesh['head'=8,'batch'=32] {'batch'}, dimensions={0} | all-to-all | bytes 1048576 | tf_op jit(solution)/shard_map/all_to_all | solution.py:313
  69.8 0.9 %shard_map.116 = (bf16[64,512]{1,0:T(8,128)(2,1)S(1)}, f32[64,512]{1,0:T(8,128)S(1)}, s32[1,1]{1,0:T(1,128)}) custom-call(bf16[512,512]{1,0:T(8,128)(2,1)S(1)} %bitcast.62, bf16[8,16,1024]{2,1,0:T(8,128)(2,1)S(1)} %all_to_all.27.parts_ref, s32[1,64]{1,0:T(1,128)S(1)} %copy-done.1), custom_call_target="tpu_custom_call" | custom-call | flops 33554432 | bytes 1048576 | tf_op jit(solution)/shard_map/pallas_call | solution.py:283
  71.4 0.2 conditional.1
  71.7 0.0 copy-start.6
  71.7 0.6 copy-done.6
  (6 shorter events, 0.0 us)
Async XLA Ops:
  0.0 34.8 %copy-start.2 = (bf16[16,512,64]{1,2,0:T(8,128)(2,1)S(1)}, bf16[16,512,64]{1,2,0:T(8,128)(2,1)}, u32[]{:S(2)}) copy-start(bf16[16,512,64]{1,2,0:T(8,128)(2,1)} %param.22) | copy-start | bytes 3145732
  6.1 41.2 %copy-start.3 = (bf16[16,64,512]{2,1,0:T(8,128)(2,1)S(1)}, bf16[16,64,512]{2,1,0:T(8,128)(2,1)}, u32[]{:S(2)}) copy-start(bf16[16,64,512]{2,1,0:T(8,128)(2,1)} %param.23) | copy-start | bytes 3145732
  6.1 28.7 %all-to-all-start.3 = ((bf16[32,16,512]{2,1,0:T(8,128)(2,1)}), bf16[32,16,512]{2,1,0:T(8,128)(2,1)S(1)}, u32[]{:S(2)}, u32[]{:S(2)}) async-start(bf16[32,16,512]{2,1,0:T(8,128)(2,1)} %bitcast.68), calls=%async_computation.3 | async-start | bytes 1048576 | tf_op jit(solution)/shard_map/all_to_all | solution.py:313
  17.7 2.2 %copy-start = (bf16[512,4096]{1,0:T(8,128)(2,1)S(1)}, bf16[512,4096]{1,0:T(8,128)(2,1)}, u32[]{:S(2)}) copy-start(bf16[512,4096]{1,0:T(8,128)(2,1)} %weight_ref.1) | copy-start | bytes 12582916
  19.9 49.9 %copy-start.1 = (s32[1,64]{1,0:T(1,128)S(1)}, s32[1,64]{1,0:T(1,128)}, u32[]{:S(2)}) copy-start(s32[1,64]{1,0:T(1,128)} %get-tuple-element.51.target_ref) | copy-start | bytes 772
  21.3 50.1 %copy-start.4 = (s32[1,32]{1,0:T(1,128)S(1)}, s32[1,32]{1,0:T(1,128)}, u32[]{:S(2)}) copy-start(s32[1,32]{1,0:T(1,128)} %list_hbm.1) | copy-start | bytes 388
  21.3 50.1 %copy-start.5 = (s32[64]{0:T(128)S(1)}, s32[64]{0:T(128)}, u32[]{:S(2)}) copy-start(s32[64]{0:T(128)} %param.19) | copy-start | bytes 772
  21.3 1.6 %collective-permute-start = (bf16[8,32,512]{2,1,0:T(8,128)(2,1)S(1)}, bf16[8,32,512]{2,1,0:T(8,128)(2,1)S(1)}, u32[]{:S(2)}, u32[]{:S(2)}) collective-permute-start(bf16[8,32,512]{2,1,0:T(8,128)(2,1)S(1)} %get-tuple-element.44), channel_id=1, source_target_pairs={{0,32},{32,0},{64,96},{96,64},{128,160},{160,128},{192,224},{224,1... | collective-permute-start | bytes 786440 | tf_op jit(solution)/shard_map/ppermute | solution.py:438
  23.6 5.6 %collective-permute-start.1 = (bf16[8,16,512]{2,1,0:T(8,128)(2,1)S(1)}, bf16[8,16,512]{2,1,0:T(8,128)(2,1)S(1)}, u32[]{:S(2)}, u32[]{:S(2)}) collective-permute-start(bf16[8,16,512]{2,1,0:T(8,128)(2,1)S(1)} %get-tuple-element.46), channel_id=1, source_target_pairs={{0,64},{32,96},{64,0},{96,32},{128,192},{160,224},{192,128},{224,1... | collective-permute-start | bytes 393224 | tf_op jit(solution)/shard_map/ppermute | solution.py:442
  71.7 0.6 copy-start.6

commit v6 on v5

--- a/solution.py
+++ b/solution.py
@@ -172,25 +172,29 @@
 
 
 def base_kernel(place_ref, attention_ref, weight_ref, keep_ref, give_ref):
-    heads, half, output_width = keep_ref.shape
+    count, _, output_width = keep_ref.shape
     first = place_ref[0, 0] == 0
     attention = attention_ref[...]
-    for h in range(heads):
-        product = nn(attention, weight_ref[:, h * output_width : (h + 1) * output_width])
-        keep_ref[h] = jnp.where(first, product[:half], product[half:]).astype(BF16)
-        give_ref[h] = jnp.where(first, product[half:], product[:half]).astype(BF16)
+    for n in range(count):
+        one = nn(attention, weight_ref[:, 2 * n * output_width : (2 * n + 1) * output_width])
+        two = nn(attention, weight_ref[:, (2 * n + 1) * output_width : (2 * n + 2) * output_width])
+        keep_ref[n] = jnp.where(first, one, two).astype(BF16)
+        give_ref[n] = jnp.where(first, two, one).astype(BF16)
 
 
 def pair_kernel(place_ref, keep_ref, sibling_ref, keep_out_ref, give_out_ref):
-    heads, quarter, _ = keep_out_ref.shape
+    count = keep_out_ref.shape[0]
     first = place_ref[0, 1] == 0
-    for h in range(heads):
-        both = keep_ref[h].astype(F32) + sibling_ref[h].astype(F32)
-        keep_out_ref[h] = jnp.where(first, both[:quarter], both[quarter:]).astype(BF16)
-        give_out_ref[h] = jnp.where(first, both[quarter:], both[:quarter]).astype(BF16)
-
-
-def home_down_kernel(got_ref, down_ref, keep_ref, other_ref, parts_ref, closing_ref, local_ref, over_ref):
+    for n in range(count):
+        one = keep_ref[2 * n].astype(F32) + sibling_ref[2 * n].astype(F32)
+        two = keep_ref[2 * n + 1].astype(F32) + sibling_ref[2 * n + 1].astype(F32)
+        keep_out_ref[n] = jnp.where(first, one, two).astype(BF16)
+        give_out_ref[n] = jnp.where(first, two, one).astype(BF16)
+
+
+def home_down_kernel(
+    place_ref, got_ref, down_ref, keep_ref, other_ref, part_ref, keep_out_ref, give_out_ref, closing_ref, local_ref, over_ref
+):
     slots, width = got_ref.shape
     peers = slots // BLOCK
     got = got_ref[...]
@@ -218,28 +222,26 @@
     total = jnp.zeros((rank, HOME_ROWS), F32)
     for n in range(16):
         total = total + jnp.where(local_lanes == n + 1.0, per_map[n * rank : (n + 1) * rank, :], 0.0)
-    total = total.astype(BF16)
-    heads, quarter, output_width = keep_ref.shape
-    total = jnp.concatenate([total[n * quarter : (n + 1) * quarter] for n in range(4)], axis=1)
-    for h in range(heads):
-        both = keep_ref[h].astype(F32) + other_ref[h].astype(F32)
-        parts_ref[h, :, :output_width] = both.astype(BF16)
-        parts_ref[h, :, output_width:] = total
+    part_ref[...] = total
+    first = place_ref[0, 2] == 0
+    one = keep_ref[0].astype(F32) + other_ref[0].astype(F32)
+    two = keep_ref[1].astype(F32) + other_ref[1].astype(F32)
+    keep_out_ref[...] = jnp.where(first, one, two)
+    give_out_ref[...] = jnp.where(first, two, one).astype(BF16)
     any_pair = jnp.max(jnp.max(flags, axis=1, keepdims=True), axis=0, keepdims=True)
     served = jnp.sum(filled, axis=0, keepdims=True)
     over = jnp.maximum(any_pair, (served > HOME_ROWS).astype(F32))
     over_ref[...] = jnp.broadcast_to(over, over_ref.shape)
 
 
-def home_up_kernel(parts_ref, up_ref, closing_ref, local_ref, over_ref, back_ref):
-    heads, quarter, wide = parts_ref.shape
-    rank = 4 * quarter
-    width = wide - 4 * HOME_ROWS
-    slots = closing_ref.shape[1]
-    total = parts_ref[0, :, width:].astype(F32)
-    for h in range(1, heads):
-        total = total + parts_ref[h, :, width:].astype(F32)
-    total = jnp.concatenate([total[:, n * HOME_ROWS : (n + 1) * HOME_ROWS] for n in range(4)], axis=0)
+def add_kernel(one_ref, two_ref, out_ref):
+    out_ref[...] = one_ref[...] + two_ref[...]
+
+
+def home_up_kernel(one_ref, two_ref, up_ref, closing_ref, local_ref, over_ref, back_ref):
+    rank = one_ref.shape[0]
+    slots, width = closing_ref.shape[1], up_ref.shape[1]
+    total = one_ref[...] + two_ref[...]
     ranked = jnp.concatenate([total, total], axis=0).T
     local = local_ref[...]
     stored = up_ref.shape[0] // rank
@@ -255,16 +257,10 @@
     back_ref[...] = jnp.where(row % BLOCK == BLOCK - 1, over_ref[:1, :1], back).astype(BF16)
 
 
-def tail_kernel(back_ref, parts_ref, target_ref, out_ref, base_ref, over_ref):
-    heads = parts_ref.shape[0]
+def tail_kernel(back_ref, keep_ref, far_ref, target_ref, out_ref, base_ref, over_ref):
     rows = target_ref.shape[1]
     slots, width = back_ref.shape
-    base = [
-        parts_ref[2 * side + core, :, :width].astype(F32) + parts_ref[heads // 2 + 2 * side + core, :, :width].astype(F32)
-        for core in range(2)
-        for side in range(2)
-    ]
-    base = jnp.concatenate(base, axis=0)
+    base = keep_ref[...] + far_ref[...].astype(F32)
     target = column(target_ref[...].astype(F32))
     picked = (iota((rows, slots), 1).astype(F32) == target).astype(F32).astype(BF16)
     back = back_ref[...]
@@ -424,42 +420,52 @@
     )
     got = exchange(send.reshape(peers, BLOCK, width), "batch").reshape(slots, width)
 
-    half, quarter = rows // 2, rows // 4
     head = lax.axis_index("head").astype(I32)
-    place = jnp.stack([head & 1, (head >> 1) & 1]).reshape(1, 2)
+    place = jnp.stack([head & 1, (head >> 1) & 1, (head >> 2) & 1]).reshape(1, 3)
+    crossing = [[(h, h ^ bit) for h in range(heads)] for bit in (1, 2, 4)]
     keep, give = call(
         base_kernel,
-        [((heads, half, output_width), BF16)] * 2,
+        [((heads // 2, rows, output_width), BF16)] * 2,
         [place, attention, output_projection_weight],
         smem=(0,),
         flops=2 * rows * width * heads * output_width,
         mib=12,
     )
-    sibling = lax.ppermute(give, "head", [(h, h ^ 1) for h in range(heads)])
+    sibling = lax.ppermute(give, "head", crossing[0])
     keep, give = call(
-        pair_kernel, [((heads, quarter, output_width), BF16)] * 2, [place, keep, sibling], smem=(0,), flops=1 << 20
-    )
-    other = lax.ppermute(give, "head", [(h, h ^ 2) for h in range(heads)])
-
-    wide = output_width + 4 * HOME_ROWS
-    parts, closing, local, over = call(
+        pair_kernel, [((heads // 4, rows, output_width), BF16)] * 2, [place, keep, sibling], smem=(0,), flops=1 << 20
+    )
+    other = lax.ppermute(give, "head", crossing[1])
+
+    part, keep, give, closing, local, over = call(
         home_down_kernel,
-        [((heads, quarter, wide), BF16), ((HOME_ROWS, slots), BF16), ((HOME_ROWS, HOME_ROWS), F32), ((8, 128), F32)],
-        [got, jnp.swapaxes(adapter_down_weight, 1, 2).reshape(stored * rank, width), keep, other],
+        [
+            ((rank, HOME_ROWS), F32),
+            ((rows, output_width), F32),
+            ((rows, output_width), BF16),
+            ((HOME_ROWS, slots), BF16),
+            ((HOME_ROWS, HOME_ROWS), F32),
+            ((8, 128), F32),
+        ],
+        [place, got, jnp.swapaxes(adapter_down_weight, 1, 2).reshape(stored * rank, width), keep, other],
+        smem=(0,),
         flops=2 * HOME_ROWS * width * stored * rank,
     )
-    parts = exchange(parts, "head")
+    for bit in range(2):
+        (part,) = call(add_kernel, [((rank, HOME_ROWS), F32)], [part, lax.ppermute(part, "head", crossing[bit])])
+    last = lax.ppermute(part, "head", crossing[2])
+    last, far = lax.optimization_barrier((last, lax.ppermute(give, "head", crossing[2])))
     (back,) = call(
         home_up_kernel,
         [((slots, output_width), BF16)],
-        [parts, adapter_up_weight.reshape(stored * rank, output_width), closing, local, over],
+        [part, last, adapter_up_weight.reshape(stored * rank, output_width), closing, local, over],
         flops=2 * HOME_ROWS * output_width * stored * rank,
     )
     back = exchange(back.reshape(peers, BLOCK, output_width), "batch").reshape(slots, output_width)
     out, base, over = call(
         tail_kernel,
         [((rows, output_width), BF16), ((rows, output_width), F32), ((1, 1), I32)],
-        [back, parts, target],
+        [back, keep, far, target],
         smem_out=(2,),
         flops=2 * rows * slots * output_width,
     )

time: 72.6 us -> 71.6 us (0.986)
  blocking collectives: 33.4 us -> 20.9 us
  starting transfers between devices: 13.2 us -> 20.5 us
  waiting for transfers between devices: 11.2 us -> 14.9 us
    all_to_all x2 -> x1, blocking collectives: 33.4 us -> 20.9 us  [exchange(): return lax.all_to_all(blocks, axis, split_axis=0, concat_axis=0, tiled=True)]
    ppermute x2 -> x6, starting transfers between devices: 1.67 us -> 9.03 us  [the longest x1 3.04 us: per_device(): last = lax.ppermute(part, 'head', crossing[2])]
    ppermute x2 -> x6, waiting for transfers between devices: 5.57 us -> 9.23 us  [the longest x1 4.05 us: per_device(): other = lax.ppermute(give, 'head', crossing[1])]
    pallas_call x6 -> x8, Pallas kernels: 10.6 us -> 11.1 us  [call(): pl.pallas_call(body, out_shape=[jax.ShapeDtypeStruct(shape, kind) for sha...]
  transfers between devices with their start and end apart: 3 -> 7, of which waited for: 3 -> 5; matrix products, arithmetic and copies ran while one was open for 0% -> 0% of each run, Pallas kernels for 3% -> 3%
where the time goes in v6:
time: 71.6 us; the launch traced here: 71.3 us
  blocking collectives  20.9 us (29%)
  starting transfers between devices  20.5 us (29%)
  waiting for transfers between devices  14.9 us (21%)
  Pallas kernels  11.1 us (16%)
  local copies, waits for them, and re-layouts  2.83 us (4%)
  between operations  0.78 us (1%)
    all_to_all x1, blocking collectives, exchange(): return lax.all_to_all(blocks, axis, split_axis=0, concat_axis=0, tiled=True)  20.9 us
    all_to_all x1, starting transfers between devices, exchange(): return lax.all_to_all(blocks, axis, split_axis=0, concat_axis=0, tiled=True)  11.5 us
    pallas_call x8, Pallas kernels, call(): pl.pallas_call(body, out_shape=[jax.ShapeDtypeStruct(shape, kind) for sha...  11.1 us
    all_to_all x1, waiting for transfers between devices, exchange(): return lax.all_to_all(blocks, axis, split_axis=0, concat_axis=0, tiled=True)  5.64 us
    ppermute x1, waiting for transfers between devices, per_device(): other = lax.ppermute(give, 'head', crossing[1])  4.05 us
    ppermute x1, starting transfers between devices, per_device(): last = lax.ppermute(part, 'head', crossing[2])  3.04 us
    unnamed x14, local copies, waits for them, and re-layouts  2.83 us
    ppermute x1, starting transfers between devices, per_device(): lax.ppermute(give, 'head', crossing[2])  2.71 us
  transfers between devices with their start and end apart: 7, of which 5 were waited for; matrix products, arithmetic and copies ran while one was open for 0% of the time, Pallas kernels for 3%

profile of v6, /device:TPU:32, one launch (start us, length us, event | category | flops | bytes accessed | tf_op | source)
XLA Modules:
  0.0 71.3 jit_solution(10843974829329601452)
XLA Ops:
  0.0 6.1 %shard_map.111 = (bf16[512,512]{1,0:T(8,128)(2,1)}, bf16[64,512]{1,0:T(8,128)(2,1)S(1)}, s32[1,64]{1,0:T(1,128)}) custom-call(s32[1,512]{1,0:T(1,128)} %index_hbm.1, s32[1,64]{1,0:T(1,128)} %count_hbm.1, s32[1,64]{1,0:T(1,128)} %bitcast.73, s32[1,64]{1,0:T(1,128)} %bitcast.74, s32[1,32]{1,0:T(1,128)} %list_hbm.1, bf16[64,512]{1,0:T(8,128)(2,1)} %q_hbm.1, ...), custom_call_target="tpu_custom_call" | custom-call | flops 1073741824 | bytes 1048576 | tf_op jit(solution)/shard_map/pallas_call | solution.py:279
  6.1 0.0 copy-start.2
  6.1 11.5 %all-to-all-start.3 = ((bf16[32,16,512]{2,1,0:T(8,128)(2,1)}), bf16[32,16,512]{2,1,0:T(8,128)(2,1)S(1)}, u32[]{:S(2)}, u32[]{:S(2)}) async-start(bf16[32,16,512]{2,1,0:T(8,128)(2,1)} %bitcast.69), calls=%async_computation.3 | async-start | bytes 1048576 | tf_op jit(solution)/shard_map/all_to_all | solution.py:309
  17.7 0.1 add_bitcast_fusion.place_ref
  17.7 2.2 %copy-done = bf16[512,4096]{1,0:T(8,128)(2,1)S(1)} copy-done((bf16[512,4096]{1,0:T(8,128)(2,1)S(1)}, bf16[512,4096]{1,0:T(8,128)(2,1)}, u32[]{:S(2)}) %copy-start) | copy-done | bytes 4194328
  19.9 1.4 %shard_map.112 = (bf16[4,64,512]{2,1,0:T(8,128)(2,1)S(1)}, bf16[4,64,512]{2,1,0:T(8,128)(2,1)S(1)}) custom-call(s32[1,3]{1,0:T(1,128)S(1)} %add_bitcast_fusion.place_ref, bf16[64,512]{1,0:T(8,128)(2,1)S(1)} %get-tuple-element.46.attention_ref, bf16[512,4096]{1,0:T(8,128)(2,1)S(1)} %copy-done), custom_call_target="tpu_custom_call" | custom-call | flops 268435456 | bytes 1048576 | tf_op jit(solution)/shard_map/pallas_call | solution.py:279
  21.3 0.1 collective-permute-start
  21.4 1.5 %collective-permute-done.sibling_ref = bf16[4,64,512]{2,1,0:T(8,128)(2,1)S(1)} collective-permute-done((bf16[4,64,512]{2,1,0:T(8,128)(2,1)S(1)}, bf16[4,64,512]{2,1,0:T(8,128)(2,1)S(1)}, u32[]{:S(2)}, u32[]{:S(2)}) %collective-permute-start) | collective-permute-done | bytes 262176 | tf_op jit(solution)/shard_map/ppermute | solution.py:434
  22.9 0.6 shard_map.113
  23.6 1.6 %collective-permute-start.1 = (bf16[2,64,512]{2,1,0:T(8,128)(2,1)S(1)}, bf16[2,64,512]{2,1,0:T(8,128)(2,1)S(1)}, u32[]{:S(2)}, u32[]{:S(2)}) collective-permute-start(bf16[2,64,512]{2,1,0:T(8,128)(2,1)S(1)} %get-tuple-element.50), channel_id=1, source_target_pairs={{0,64},{32,96},{64,0},{96,32},{128,192},{160,224},{192,128},{224,1... | collective-permute-start | bytes 393224 | tf_op jit(solution)/shard_map/ppermute | solution.py:438
  25.1 4.0 %collective-permute-done.1.other_ref = bf16[2,64,512]{2,1,0:T(8,128)(2,1)S(1)} collective-permute-done((bf16[2,64,512]{2,1,0:T(8,128)(2,1)S(1)}, bf16[2,64,512]{2,1,0:T(8,128)(2,1)S(1)}, u32[]{:S(2)}, u32[]{:S(2)}) %collective-permute-start.1) | collective-permute-done | bytes 131104 | tf_op jit(solution)/shard_map/ppermute | solution.py:438
  29.2 5.6 %all-to-all-done.3 = bf16[32,16,512]{2,1,0:T(8,128)(2,1)S(1)} async-done(((bf16[32,16,512]{2,1,0:T(8,128)(2,1)}), bf16[32,16,512]{2,1,0:T(8,128)(2,1)S(1)}, u32[]{:S(2)}, u32[]{:S(2)}) %all-to-all-start.3) | async-done | bytes 524320 | tf_op jit(solution)/shard_map/all_to_all | solution.py:309
  34.8 1.4 %shard_map.114 = (f32[64,128]{1,0:T(8,128)S(1)}, f32[64,512]{1,0:T(8,128)S(1)}, bf16[64,512]{1,0:T(8,128)(2,1)S(1)}, bf16[128,512]{1,0:T(8,128)(2,1)S(1)}, f32[128,128]{1,0:T(8,128)S(1)}, /*index=5*/f32[8,128]{1,0:T(8,128)S(1)}) custom-call(s32[1,3]{1,0:T(1,128)S(1)} %add_bitcast_fusion.place_ref, bf16[512,512]{1,0:T(8,128)(2,1)S(1)} %bitcast.64, ...), custom_call_target="tpu_custom_call" | custom-call | flops 134217728 | bytes 1048576 | tf_op jit(solution)/shard_map/pallas_call | solution.py:279
  36.3 0.1 collective-permute-start.2
  36.4 1.2 %collective-permute-done.2.two_ref = f32[64,128]{1,0:T(8,128)S(1)} collective-permute-done((f32[64,128]{1,0:T(8,128)S(1)}, f32[64,128]{1,0:T(8,128)S(1)}, u32[]{:S(2)}, u32[]{:S(2)}) %collective-permute-start.2) | collective-permute-done | bytes 32800 | tf_op jit(solution)/shard_map/ppermute | solution.py:455
  37.6 1.5 %collective-permute-start.3 = (f32[64,128]{1,0:T(8,128)S(1)}, f32[64,128]{1,0:T(8,128)S(1)}, u32[]{:S(2)}, u32[]{:S(2)}) collective-permute-start(f32[64,128]{1,0:T(8,128)S(1)} %shard_map.115.one_ref), channel_id=1, source_target_pairs={{0,64},{32,96},{64,0},{96,32},{128,192},{160,224},{192,128},{224,1... | collective-permute-start | bytes 98312 | tf_op jit(solution)/shard_map/ppermute | solution.py:455
  39.1 2.7 %collective-permute-start.5 = (bf16[64,512]{1,0:T(8,128)(2,1)S(1)}, bf16[64,512]{1,0:T(8,128)(2,1)S(1)}, u32[]{:S(2)}, u32[]{:S(2)}) collective-permute-start(bf16[64,512]{1,0:T(8,128)(2,1)S(1)} %get-tuple-element.52), channel_id=1, source_target_pairs={{0,128},{32,160},{64,192},{96,224},{128,0},{160,32},{192,64},{224,... | collective-permute-start | bytes 196616 | tf_op jit(solution)/shard_map/ppermute | solution.py:457
  41.8 3.0 %collective-permute-start.4 = (f32[64,128]{1,0:T(8,128)S(1)}, f32[64,128]{1,0:T(8,128)S(1)}, u32[]{:S(2)}, u32[]{:S(2)}) collective-permute-start(f32[64,128]{1,0:T(8,128)S(1)} %shard_map.116.one_ref), channel_id=1, source_target_pairs={{0,128},{32,160},{64,192},{96,224},{128,0},{160,32},{192,64},{224,... | collective-permute-start | bytes 98312 | tf_op jit(solution)/shard_map/ppermute | solution.py:456
  44.9 2.5 %collective-permute-done.4.two_ref = f32[64,128]{1,0:T(8,128)S(1)} collective-permute-done((f32[64,128]{1,0:T(8,128)S(1)}, f32[64,128]{1,0:T(8,128)S(1)}, u32[]{:S(2)}, u32[]{:S(2)}) %collective-permute-start.4) | collective-permute-done | bytes 32800 | tf_op jit(solution)/shard_map/ppermute | solution.py:456
  47.3 0.6 shard_map.117
  48.0 20.9 %all_to_all.22 = bf16[32,16,512]{2,1,0:T(8,128)(2,1)S(1)} all-to-all(bf16[32,16,512]{2,1,0:T(8,128)(2,1)S(1)} %bitcast.62), channel_id=1, replica_groups=mesh['head'=8,'batch'=32] {'batch'}, dimensions={0} | all-to-all | bytes 1048576 | tf_op jit(solution)/shard_map/all_to_all | solution.py:309
  68.9 0.9 %shard_map.118 = (bf16[64,512]{1,0:T(8,128)(2,1)S(1)}, f32[64,512]{1,0:T(8,128)S(1)}, s32[1,1]{1,0:T(1,128)}) custom-call(bf16[512,512]{1,0:T(8,128)(2,1)S(1)} %bitcast.63, f32[64,512]{1,0:T(8,128)S(1)} %get-tuple-element.57.keep_ref, bf16[64,512]{1,0:T(8,128)(2,1)S(1)} %collective-permute-done.5.far_ref, s32[1,64]{1,0:T(1,128)S(1)} %copy-done.1), custom_call_target="tpu_custom_call" | custom-call | flops 33554432 | bytes 1048576 | tf_op jit(solution)/shard_map/pallas_call | solution.py:279
  70.5 0.2 conditional.1
  70.7 0.6 copy-done.6
  (15 shorter events, 0.0 us)
Async XLA Ops:
  0.0 34.8 %copy-start.3 = (bf16[16,512,64]{1,2,0:T(8,128)(2,1)S(1)}, bf16[16,512,64]{1,2,0:T(8,128)(2,1)}, u32[]{:S(2)}) copy-start(bf16[16,512,64]{1,2,0:T(8,128)(2,1)} %param.22) | copy-start | bytes 3145732
  6.1 41.2 %copy-start.2 = (bf16[16,64,512]{2,1,0:T(8,128)(2,1)S(1)}, bf16[16,64,512]{2,1,0:T(8,128)(2,1)}, u32[]{:S(2)}) copy-start(bf16[16,64,512]{2,1,0:T(8,128)(2,1)} %param.23) | copy-start | bytes 3145732
  6.1 28.7 %all-to-all-start.3 = ((bf16[32,16,512]{2,1,0:T(8,128)(2,1)}), bf16[32,16,512]{2,1,0:T(8,128)(2,1)S(1)}, u32[]{:S(2)}, u32[]{:S(2)}) async-start(bf16[32,16,512]{2,1,0:T(8,128)(2,1)} %bitcast.69), calls=%async_computation.3 | async-start | bytes 1048576 | tf_op jit(solution)/shard_map/all_to_all | solution.py:309
  17.7 2.2 %copy-start = (bf16[512,4096]{1,0:T(8,128)(2,1)S(1)}, bf16[512,4096]{1,0:T(8,128)(2,1)}, u32[]{:S(2)}) copy-start(bf16[512,4096]{1,0:T(8,128)(2,1)} %weight_ref.1) | copy-start | bytes 12582916
  19.9 49.0 %copy-start.1 = (s32[1,64]{1,0:T(1,128)S(1)}, s32[1,64]{1,0:T(1,128)}, u32[]{:S(2)}) copy-start(s32[1,64]{1,0:T(1,128)} %get-tuple-element.59.target_ref) | copy-start | bytes 772
  19.9 50.5 %copy-start.4 = (s32[1,32]{1,0:T(1,128)S(1)}, s32[1,32]{1,0:T(1,128)}, u32[]{:S(2)}) copy-start(s32[1,32]{1,0:T(1,128)} %list_hbm.1) | copy-start | bytes 388
  19.9 50.5 %copy-start.5 = (s32[64]{0:T(128)S(1)}, s32[64]{0:T(128)}, u32[]{:S(2)}) copy-start(s32[64]{0:T(128)} %param.19) | copy-start | bytes 772
  21.3 1.6 %collective-permute-start = (bf16[4,64,512]{2,1,0:T(8,128)(2,1)S(1)}, bf16[4,64,512]{2,1,0:T(8,128)(2,1)S(1)}, u32[]{:S(2)}, u32[]{:S(2)}) collective-permute-start(bf16[4,64,512]{2,1,0:T(8,128)(2,1)S(1)} %get-tuple-element.48), channel_id=1, source_target_pairs={{0,32},{32,0},{64,96},{96,64},{128,160},{160,128},{192,224},{224,1... | collective-permute-start | bytes 786440 | tf_op jit(solution)/shard_map/ppermute | solution.py:434
  23.6 5.6 %collective-permute-start.1 = (bf16[2,64,512]{2,1,0:T(8,128)(2,1)S(1)}, bf16[2,64,512]{2,1,0:T(8,128)(2,1)S(1)}, u32[]{:S(2)}, u32[]{:S(2)}) collective-permute-start(bf16[2,64,512]{2,1,0:T(8,128)(2,1)S(1)} %get-tuple-element.50), channel_id=1, source_target_pairs={{0,64},{32,96},{64,0},{96,32},{128,192},{160,224},{192,128},{224,1... | collective-permute-start | bytes 393224 | tf_op jit(solution)/shard_map/ppermute | solution.py:438
  36.3 1.3 %collective-permute-start.2 = (f32[64,128]{1,0:T(8,128)S(1)}, f32[64,128]{1,0:T(8,128)S(1)}, u32[]{:S(2)}, u32[]{:S(2)}) collective-permute-start(f32[64,128]{1,0:T(8,128)S(1)} %get-tuple-element.51.one_ref), channel_id=1, source_target_pairs={{0,32},{32,0},{64,96},{96,64},{128,160},{160,128},{192,224},{224,1... | collective-permute-start | bytes 98312 | tf_op jit(solution)/shard_map/ppermute | solution.py:455
  37.6 4.2 %collective-permute-start.3 = (f32[64,128]{1,0:T(8,128)S(1)}, f32[64,128]{1,0:T(8,128)S(1)}, u32[]{:S(2)}, u32[]{:S(2)}) collective-permute-start(f32[64,128]{1,0:T(8,128)S(1)} %shard_map.115.one_ref), channel_id=1, source_target_pairs={{0,64},{32,96},{64,0},{96,32},{128,192},{160,224},{192,128},{224,1... | collective-permute-start | bytes 98312 | tf_op jit(solution)/shard_map/ppermute | solution.py:455
  39.1 5.8 %collective-permute-start.5 = (bf16[64,512]{1,0:T(8,128)(2,1)S(1)}, bf16[64,512]{1,0:T(8,128)(2,1)S(1)}, u32[]{:S(2)}, u32[]{:S(2)}) collective-permute-start(bf16[64,512]{1,0:T(8,128)(2,1)S(1)} %get-tuple-element.52), channel_id=1, source_target_pairs={{0,128},{32,160},{64,192},{96,224},{128,0},{160,32},{192,64},{224,... | collective-permute-start | bytes 196616 | tf_op jit(solution)/shard_map/ppermute | solution.py:457
  41.8 5.5 %collective-permute-start.4 = (f32[64,128]{1,0:T(8,128)S(1)}, f32[64,128]{1,0:T(8,128)S(1)}, u32[]{:S(2)}, u32[]{:S(2)}) collective-permute-start(f32[64,128]{1,0:T(8,128)S(1)} %shard_map.116.one_ref), channel_id=1, source_target_pairs={{0,128},{32,160},{64,192},{96,224},{128,0},{160,32},{192,64},{224,... | collective-permute-start | bytes 98312 | tf_op jit(solution)/shard_map/ppermute | solution.py:456
  70.7 0.6 copy-start.6
